TPU v7x, 32 devices: a whole 2x2x4 slice. The times are simulated.
32 devices in a mesh: rep: 4 (over x, y), dp: 8 (over z, core).
Axes of the slice: x: 2, y: 2, z: 4, core: 2. Of those that a mesh axis runs over, the one named last changes fastest.
Arguments:
- x: bfloat16 [32, 4096, 768], P(('rep', 'dp')), parts along dimension 0
- dy: bfloat16 [32, 4096, 768], P(('rep', 'dp')), parts along dimension 0
- w_gate: bfloat16 [2, 768, 1792], P(None, 'dp')
- w_up: bfloat16 [2, 768, 1792], P(None, 'dp')
- w_down: bfloat16 [2, 1792, 768], P(None, 'dp')
- m_w_gate: float32 [2, 768, 1792], P(None, 'dp')
- m_w_up: float32 [2, 768, 1792], P(None, 'dp')
- m_w_down: float32 [2, 1792, 768], P(None, 'dp')
- v_w_gate: float32 [2, 768, 1792], P(None, 'dp')
- v_w_up: float32 [2, 768, 1792], P(None, 'dp')
- v_w_down: float32 [2, 1792, 768], P(None, 'dp')
Outputs:
- output 1: bfloat16 [8, 768, 1792], P('rep', 'dp'), parts along dimension 0
- output 2: bfloat16 [8, 768, 1792], P('rep', 'dp'), parts along dimension 0
- output 3: bfloat16 [8, 1792, 768], P('rep', 'dp'), parts along dimension 0
- output 4: float32 [8, 768, 1792], P('rep', 'dp'), parts along dimension 0
- output 5: float32 [8, 768, 1792], P('rep', 'dp'), parts along dimension 0
- output 6: float32 [8, 1792, 768], P('rep', 'dp'), parts along dimension 0
- output 7: float32 [8, 768, 1792], P('rep', 'dp'), parts along dimension 0
- output 8: float32 [8, 768, 1792], P('rep', 'dp'), parts along dimension 0
- output 9: float32 [8, 1792, 768], P('rep', 'dp'), parts along dimension 0
There are 4 independent parts. A program takes and returns all parts, laid end to end along the dimension named above; an argument that names none is the same for every part.
All inputs are finite; a program needn't handle non-finite values.
Results may differ from a plain program's by a relative error of at most 0.022.
Values are sent between devices in bfloat16 or wider.
A program may use at most 2 GiB of HBM per device.

v0:
```python
import jax
import jax.numpy as jnp
from jax import lax
from jax.sharding import PartitionSpec as P

NAMES = ("w_gate", "w_up", "w_down")


def matmul(a, w):
    return jnp.dot(a, w, preferred_element_type=jnp.float32).astype(jnp.bfloat16)


def normed(h):
    wide = h.astype(jnp.float32)
    scale = lax.rsqrt(jnp.mean(wide**2, -1, keepdims=True) + 1e-6)
    return (wide * scale).astype(jnp.bfloat16)


def layer(h, w):
    a = normed(h)
    gate = jnp.dot(a, w["w_gate"], preferred_element_type=jnp.float32)
    up = jnp.dot(a, w["w_up"], preferred_element_type=jnp.float32)
    return h + matmul((jax.nn.silu(gate) * up).astype(jnp.bfloat16), w["w_down"])


def adamw(w, m, v, g):
    m = 0.9 * m + 0.1 * g
    v = 0.95 * v + 0.05 * g * g
    step = m * lax.rsqrt(v + 1e-8) + 0.1 * w
    return (w - 0.02 * step).astype(jnp.bfloat16), m, v


def clipped(gradients, sum_of_squares, count):
    factor = jnp.minimum(1.0, 0.5 * lax.rsqrt(sum_of_squares / count + 1e-30))
    return [g * factor for g in gradients]


def solution(mesh):
    def fetched(weights, number):
        return {name: lax.all_gather(w[number], "dp", axis=0, tiled=True) for name, w in zip(NAMES, weights, strict=True)}

    def step(x, dy, *arrays):
        weights, m, v = (arrays[i : i + 3] for i in (0, 3, 6))
        layers = weights[0].shape[0]
        h, kept = x[0], []
        for number in range(layers):
            kept.append(h)
            h = layer(h, fetched(weights, number))
        by_h, mine = dy[0], [None] * layers
        for number in reversed(range(layers)):
            _, back = jax.vjp(lambda w, h: layer(h, w), fetched(weights, number), kept[number])
            by_w, by_h = back(by_h)
            mine[number] = [lax.psum_scatter(by_w[name], "dp", scatter_dimension=0, tiled=True) for name in NAMES]
        gradients = [jnp.stack([mine[number][i] for number in range(layers)]).astype(jnp.float32) for i in range(3)]
        squares = lax.psum(sum(jnp.sum(g * g) for g in gradients), "dp")
        gradients = clipped(gradients, squares, lax.psum(1, "dp") * sum(g.size for g in gradients))
        new = [adamw(w.astype(jnp.float32), m, v, g) for w, m, v, g in zip(weights, m, v, gradients, strict=True)]
        return tuple(one[which] for which in range(3) for one in new)

    states, cut = P(("rep", "dp"), None, None), P(None, "dp", None)
    return jax.shard_map(
        step,
        mesh=mesh,
        in_specs=(states, states) + (cut,) * 9,
        out_specs=(P("rep", "dp", None),) * 9,
        check_vma=False,
    )
```

profile of v0, /device:TPU:0, one launch (start us, length us, event | category | flops | bytes accessed | tf_op | source)
XLA Modules:
  0.0 618.8 jit_solution(6457017998730976944)
XLA Ops:
  7.2 0.0 all-gather.13.cloned.1.call-start
  7.2 2.0 fusion.102
  9.2 0.0 all-gather.13.cloned.1.call-update
  9.2 0.0 all-gather.15.cloned.1.call-start
  9.3 2.0 fusion.101
  11.2 0.0 all-gather.15.cloned.1.call-update
  11.3 0.0 all-gather.17.cloned.1.call-start
  11.3 2.0 fusion.100
  13.3 0.0 all-gather.17.cloned.1.call-update
  13.3 0.0 all-gather.23.cloned.1.call-start
  13.4 0.5 all-gather.23.cloned.1.call-update
  13.9 0.0 all-gather.21.cloned.1.call-start
  13.9 0.5 all-gather.21.cloned.1.call-update
  14.5 0.0 all-gather.19.cloned.1.call-start
  14.5 0.5 all-gather.19.cloned.1.call-update
  15.1 0.0 reduce-scatter.9.cloned.1.call-start
  15.1 8.7 %copy.20 = bf16[1,4096,768]{1,2,0:T(8,128)(2,1)} copy(bf16[1,4096,768]{2,1,0:T(8,128)(2,1)} %param.11) | data formatting | bytes 12582912 | tf_op args[0]
  23.8 4.1 fusion.15
  27.9 8.8 %copy.21 = bf16[1,4096,768]{1,2,0:T(8,128)(2,1)} copy(bf16[1,4096,768]{2,1,0:T(8,128)(2,1)} %param.12) | data formatting | bytes 12582912 | tf_op args[1]
  36.7 10.7 %all-gather.13.cloned.1.call-done = bf16[1,768,1792]{2,1,0:T(8,128)(2,1)} async-done(((bf16[1,96,1792]{2,1,0:T(8,128)(2,1)}), bf16[1,768,1792]{2,1,0:T(8,128)(2,1)}) %all-gather.13.cloned.1.call-update) | async-done | bytes 2752528 | tf_op jit(solution)/shard_map/all_gather | solution.py:40
  47.5 19.8 %fusion.39 = f32[4096,1792]{1,0:T(8,128)} fusion(bf16[1,4096,768]{1,2,0:T(8,128)(2,1)} %copy.20, f32[4096]{0:T(1024)S(1)} %add_rsqrt_fusion, bf16[1,768,1792]{2,1,0:T(8,128)(2,1)} %all-gather.13.cloned.1.call-done), kind=kOutput, calls=%fused_computation.52 | convolution fusion | flops 11283726336 | bytes 38420480 | tf_op jit(solution)/shard_map/dot_general | solution.py:21
  67.3 16.2 %all-gather.15.cloned.1.call-done = bf16[1,768,1792]{2,1,0:T(8,128)(2,1)} async-done(((bf16[1,96,1792]{2,1,0:T(8,128)(2,1)}), bf16[1,768,1792]{2,1,0:T(8,128)(2,1)}) %all-gather.15.cloned.1.call-update) | async-done | bytes 2752528 | tf_op jit(solution)/shard_map/all_gather | solution.py:40
  83.5 33.7 %multiply_convert_fusion.1 = (bf16[4096,1792]{1,0:T(8,128)(2,1)}, f32[4096,1792]{1,0:T(8,128)}) fusion(f32[4096,1792]{1,0:T(8,128)} %fusion.39, bf16[1,768,1792]{2,1,0:T(8,128)(2,1)} %all-gather.15.cloned.1.call-done, bf16[1,4096,768]{1,2,0:T(8,128)(2,1)} %copy.20, f32[4096]{0:T(1024)S(1)} %add_rsqrt_fusion), kind=kOutput, calls=%fused_computation.17 | convolution fusion | flops 11327766528 | bytes 82460672 | tf_op jit(solution)/shard_map/dot_general | solution.py:22
  117.2 2.3 all-gather.17.cloned.1.call-done
  119.5 19.2 %fusion.19 = (f32[4096]{0:T(1024)S(1)}, bf16[4096,768]{0,1:T(8,128)(2,1)}) fusion(bf16[4096,1792]{1,0:T(8,128)(2,1)} %get-tuple-element.24, bf16[1,1792,768]{2,1,0:T(8,128)(2,1)} %all-gather.17.cloned.1.call-done, bf16[1,4096,768]{1,2,0:T(8,128)(2,1)} %copy.20), kind=kOutput, calls=%fused_computation.37 | convolution fusion | flops 11290013696 | bytes 30031872 | tf_op jit(solution)/shard_map/dot_general | solution.py:10
  138.7 16.7 %all-gather.23.cloned.1.call-done = bf16[1,768,1792]{2,1,0:T(8,128)(2,1)} async-done(((bf16[1,96,1792]{2,1,0:T(8,128)(2,1)}), bf16[1,768,1792]{2,1,0:T(8,128)(2,1)}) %all-gather.23.cloned.1.call-update) | async-done | bytes 2752528 | tf_op jit(solution)/shard_map/all_gather | solution.py:40
  155.3 19.9 %fusion.31 = f32[4096,1792]{1,0:T(8,128)} fusion(bf16[4096,768]{0,1:T(8,128)(2,1)} %get-tuple-element.27, f32[4096]{0:T(1024)S(1)} %fusion.88, bf16[1,768,1792]{2,1,0:T(8,128)(2,1)} %all-gather.23.cloned.1.call-done), kind=kOutput, calls=%fused_computation.49 | convolution fusion | flops 11283726336 | bytes 38420480 | tf_op jit(solution)/shard_map/jvp()/dot_general | solution.py:22
  175.3 15.9 %all-gather.21.cloned.1.call-done = bf16[1,1792,768]{2,1,0:T(8,128)(2,1)} async-done(((bf16[1,224,768]{2,1,0:T(8,128)(2,1)}), bf16[1,1792,768]{2,1,0:T(8,128)(2,1)}) %all-gather.21.cloned.1.call-update) | async-done | bytes 2752528 | tf_op jit(solution)/shard_map/all_gather | solution.py:40
  191.2 17.5 %convolution_convert_fusion.1 = bf16[4096,1792]{1,0:T(8,128)(2,1)} fusion(bf16[1,4096,768]{2,1,0:T(8,128)(2,1)} %param.12, bf16[1,1792,768]{2,1,0:T(8,128)(2,1)} %all-gather.21.cloned.1.call-done), kind=kOutput, calls=%fused_computation.30 | convolution fusion | flops 11281629184 | bytes 23724032 | tf_op jit(solution)/shard_map/transpose(jvp())/dot_general | solution.py:10
  208.7 18.3 %all-gather.19.cloned.1.call-done = bf16[1,768,1792]{2,1,0:T(8,128)(2,1)} async-done(((bf16[1,96,1792]{2,1,0:T(8,128)(2,1)}), bf16[1,768,1792]{2,1,0:T(8,128)(2,1)}) %all-gather.19.cloned.1.call-update) | async-done | bytes 2752528 | tf_op jit(solution)/shard_map/all_gather | solution.py:40
  227.0 39.8 %fusion.2 = (bf16[4096,1792]{1,0:T(8,128)(2,1)}, f32[4096,1792]{1,0:T(8,128)}) fusion(f32[4096,1792]{1,0:T(8,128)} %fusion.31, bf16[4096,1792]{1,0:T(8,128)(2,1)} %convolution_convert_fusion.1, bf16[1,768,1792]{2,1,0:T(8,128)(2,1)} %all-gather.19.cloned.1.call-done, bf16[4096,768]{0,1:T(8,128)(2,1)} %get-tuple-element.27, f32[4096]{0:T(1024)S(1)} %fusion.88), kind=kOutput, calls=%fused_computation.8 | convolution fusion | flops 11371806720 | bytes 97140736 | tf_op jit(solution)/shard_map/jvp()/dot_general | solution.py:21
  266.9 18.8 %fusion.49 = bf16[768,1792]{1,0:T(8,128)(2,1)} fusion(bf16[4096,1792]{1,0:T(8,128)(2,1)} %get-tuple-element.28, bf16[4096,768]{0,1:T(8,128)(2,1)} %get-tuple-element.27, f32[4096]{0:T(1024)S(1)} %fusion.88), kind=kOutput, calls=%fused_computation.56 | convolution fusion | flops 11283726336 | bytes 23740416 | tf_op jit(solution)/shard_map/transpose(jvp())/dot_general | solution.py:21
  285.6 0.0 reduce-scatter.9.cloned.1.call-update
  285.7 0.0 reduce-scatter.7.cloned.1.call-start
  285.7 23.5 %fusion.22 = bf16[4096,768]{0,1:T(8,128)(2,1)} fusion(bf16[4096,1792]{1,0:T(8,128)(2,1)} %convolution_convert_fusion.1, bf16[1,768,1792]{2,1,0:T(8,128)(2,1)} %all-gather.23.cloned.1.call-done, f32[4096,1792]{1,0:T(8,128)} %get-tuple-element.29), kind=kOutput, calls=%fused_computation.40 | convolution fusion | flops 11321475072 | bytes 53084160 | tf_op jit(solution)/shard_map/transpose(jvp())/dot_general | solution.py:22
  309.2 20.5 %fusion.21 = (f32[4096]{0:T(1024)S(1)}, bf16[4096,768]{0,1:T(8,128)(2,1)}) fusion(bf16[4096,768]{0,1:T(8,128)(2,1)} %get-tuple-element.27, bf16[4096,768]{0,1:T(8,128)(2,1)} %fusion.22, bf16[4096,1792]{1,0:T(8,128)(2,1)} %get-tuple-element.28, bf16[1,768,1792]{2,1,0:T(8,128)(2,1)} %all-gather.19.cloned.1.call-done), kind=kOutput, calls=%fused_computation.39 | convolution fusion | flops 11290013696 | bytes 36323328 | tf_op jit(solution)/shard_map/transpose(jvp())/dot_general | solution.py:21
  329.8 9.7 %fusion.23 = bf16[4096,768]{0,1:T(8,128)(2,1)} fusion(bf16[4096,768]{0,1:T(8,128)(2,1)} %get-tuple-element.27, bf16[4096,768]{0,1:T(8,128)(2,1)} %get-tuple-element.31, bf16[1,4096,768]{1,2,0:T(8,128)(2,1)S(1)} %bitcast.69, f32[4096]{0:T(1024)S(1)} %multiply_multiply_fusion.3, f32[4096]{0:T(1024)S(1)} %fusion.88), kind=kLoop, calls=%fused_computation.43 | loop fusion | flops 22020096 | bytes 25198592 | tf_op jit(solution)/shard_map/transpose(jvp())/add_any | solution.py:14
  339.5 19.7 %convolution_convert_fusion = bf16[4096,1792]{1,0:T(8,128)(2,1)} fusion(bf16[4096,768]{0,1:T(8,128)(2,1)} %fusion.23, bf16[1,1792,768]{2,1,0:T(8,128)(2,1)S(1)} %copy-done.16), kind=kOutput, calls=%fused_computation.29 | convolution fusion | flops 11281629184 | bytes 23724032 | tf_op jit(solution)/shard_map/transpose(jvp())/dot_general | solution.py:10
  359.2 30.0 %fusion.41 = bf16[768,1792]{1,0:T(8,128)(2,1)} fusion(f32[4096,1792]{1,0:T(8,128)} %fusion.39, f32[4096,1792]{1,0:T(8,128)} %get-tuple-element.25, bf16[4096,1792]{1,0:T(8,128)(2,1)} %convolution_convert_fusion, bf16[1,4096,768]{1,2,0:T(8,128)(2,1)} %copy.20, f32[4096]{0:T(1024)S(1)} %copy-done.15), kind=kOutput, calls=%fused_computation.53 | convolution fusion | flops 11365842944 | bytes 82460672 | tf_op jit(solution)/shard_map/transpose(jvp())/dot_general | solution.py:21
  389.2 0.0 reduce-scatter.7.cloned.1.call-update
  389.2 0.0 reduce-scatter.13.cloned.1.call-start
  389.3 25.5 %fusion.55 = bf16[768,1792]{1,0:T(8,128)(2,1)} fusion(bf16[4096,1792]{1,0:T(8,128)(2,1)} %convolution_convert_fusion.1, bf16[4096,768]{0,1:T(8,128)(2,1)} %get-tuple-element.27, f32[4096]{0:T(1024)S(1)} %fusion.88, f32[4096,1792]{1,0:T(8,128)} %get-tuple-element.29), kind=kOutput, calls=%fused_computation.58 | convolution fusion | flops 11329142784 | bytes 53100544 | tf_op jit(solution)/shard_map/transpose(jvp())/dot_general | solution.py:22
  414.8 0.0 reduce-scatter.11.cloned.1.call-start
  414.8 25.5 %fusion.46 = bf16[768,1792]{1,0:T(8,128)(2,1)} fusion(bf16[4096,1792]{1,0:T(8,128)(2,1)} %convolution_convert_fusion, f32[4096,1792]{1,0:T(8,128)} %fusion.39, bf16[1,4096,768]{1,2,0:T(8,128)(2,1)} %copy.20, f32[4096]{0:T(1024)S(1)} %copy-done.15), kind=kOutput, calls=%fused_computation.54 | convolution fusion | flops 11329142784 | bytes 53100544 | tf_op jit(solution)/shard_map/transpose(jvp())/dot_general | solution.py:22
  440.3 0.0 reduce-scatter.17.cloned.1.call-start
  440.4 26.0 %fusion.52 = bf16[1792,768]{1,0:T(8,128)(2,1)} fusion(bf16[1,4096,768]{2,1,0:T(8,128)(2,1)} %param.12, f32[4096,1792]{1,0:T(8,128)} %fusion.31, f32[4096,1792]{1,0:T(8,128)} %get-tuple-element.29), kind=kOutput, calls=%fused_computation.57 | convolution fusion | flops 11319705600 | bytes 67764224 | tf_op jit(solution)/shard_map/transpose(jvp())/dot_general | solution.py:10
  466.4 0.0 reduce-scatter.17.cloned.1.call-update
  466.5 0.0 reduce-scatter.15.cloned.1.call-start
  466.5 17.9 %convolution_convert_fusion.4 = bf16[1792,768]{1,0:T(8,128)(2,1)} fusion(bf16[4096,1792]{1,0:T(8,128)(2,1)} %get-tuple-element.24, bf16[4096,768]{0,1:T(8,128)(2,1)} %fusion.23), kind=kOutput, calls=%fused_computation.55 | convolution fusion | flops 11275665408 | bytes 23724032 | tf_op jit(solution)/shard_map/transpose(jvp())/dot_general | solution.py:10
  484.4 0.0 reduce-scatter.15.cloned.1.call-update
  484.5 0.0 reduce-scatter.9.cloned.1.call-done
  484.5 0.0 reduce-scatter.7.cloned.1.call-done
  484.5 2.1 fusion.76
  486.6 18.9 %reduce-scatter.11.cloned.1.call-done = bf16[96,1792]{1,0:T(8,128)(2,1)} async-done(((bf16[768,1792]{1,0:T(8,128)(2,1)}), bf16[96,1792]{1,0:T(8,128)(2,1)}) %reduce-scatter.11.cloned.1.call-update) | async-done | bytes 344080 | tf_op jit(solution)/shard_map/reduce_scatter | solution.py:53
  505.5 2.0 fusion.77
  508.8 36.2 %reduce-scatter.17.cloned.1.call-done = bf16[224,768]{1,0:T(8,128)(2,1)} async-done(((bf16[1792,768]{1,0:T(8,128)(2,1)}), bf16[224,768]{1,0:T(8,128)(2,1)}) %reduce-scatter.17.cloned.1.call-update) | async-done | bytes 344080 | tf_op jit(solution)/shard_map/reduce_scatter | solution.py:53
  545.1 39.4 %reduce-scatter.15.cloned.1.call-done = bf16[224,768]{1,0:T(8,128)(2,1)} async-done(((bf16[1792,768]{1,0:T(8,128)(2,1)}), bf16[224,768]{1,0:T(8,128)(2,1)}) %reduce-scatter.15.cloned.1.call-update) | async-done | bytes 344080 | tf_op jit(solution)/shard_map/reduce_scatter | solution.py:53
  584.4 2.0 fusion.78
  587.1 15.5 %psum.7 = f32[]{:T(128)} all-reduce(f32[]{:T(128)S(6)} %add.99), channel_id=1, replica_groups=mesh['rep'=4,'dp'=8] {'dp'}, use_global_device_ids=true, to_apply=%region_12.13 | all-reduce | flops 1 | bytes 8 | tf_op jit(solution)/shard_map/psum | solution.py:55
  603.4 3.8 fusion.84
  607.3 0.3 copy-done.9
  607.6 0.4 copy-done.10
  608.0 0.2 copy-done.11
  608.1 3.6 fusion.75
  (42 shorter events, 0.2 us)
Async XLA Ops:
  7.2 40.3 %all-gather.13.cloned.1.call-start = ((), (), s32[]{:S(2)}) async-start(), calls=%async_computation.12 | async-start | bytes 3096576 | tf_op jit(solution)/shard_map/all_gather | solution.py:40
  9.2 74.3 %all-gather.15.cloned.1.call-start = ((), (), s32[]{:S(2)}) async-start(), calls=%async_computation.13 | async-start | bytes 3096576 | tf_op jit(solution)/shard_map/all_gather | solution.py:40
  11.3 108.2 %all-gather.17.cloned.1.call-start = ((), (), s32[]{:S(2)}) async-start(), calls=%async_computation.14 | async-start | bytes 3096576 | tf_op jit(solution)/shard_map/all_gather | solution.py:40
  13.3 142.0 %all-gather.23.cloned.1.call-start = ((), (), s32[]{:S(2)}) async-start(), calls=%async_computation.17 | async-start | bytes 3096576 | tf_op jit(solution)/shard_map/all_gather | solution.py:40
  13.9 177.3 %all-gather.21.cloned.1.call-start = ((), (), s32[]{:S(2)}) async-start(), calls=%async_computation.16 | async-start | bytes 3096576 | tf_op jit(solution)/shard_map/all_gather | solution.py:40
  14.5 212.6 %all-gather.19.cloned.1.call-start = ((), (), s32[]{:S(2)}) async-start(), calls=%async_computation.15 | async-start | bytes 3096576 | tf_op jit(solution)/shard_map/all_gather | solution.py:40
  15.1 469.4 %reduce-scatter.9.cloned.1.call-start = ((), (), s32[]{:S(2)}) async-start(), calls=%async_computation.7 | async-start | bytes 3096576 | tf_op jit(solution)/shard_map/reduce_scatter | solution.py:53
  27.9 55.6 %copy-start.14 = (f32[4096]{0:T(1024)}, f32[4096]{0:T(1024)S(1)}, u32[]{:S(2)}) copy-start(f32[4096]{0:T(1024)S(1)} %add_rsqrt_fusion) | copy-start | bytes 49156
  138.7 36.6 %copy-start.12 = (f32[4096]{0:T(1024)}, f32[4096]{0:T(1024)S(1)}, u32[]{:S(2)}) copy-start(f32[4096]{0:T(1024)S(1)} %get-tuple-element.26) | copy-start | bytes 49156
  266.9 62.9 %slice-start = ((s8[6291456]{0:T(1024)(128)(4,1)}), s8[2097152]{0:T(1024)(128)(4,1)S(1)}, s32[]{:S(2)}) async-start(s8[6291456]{0:T(1024)(128)(4,1)} %bitcast.68), calls=%async_computation.18 | async-start | bytes 4194304
  285.7 198.8 %reduce-scatter.7.cloned.1.call-start = ((), (), s32[]{:S(2)}) async-start(), calls=%async_computation.6 | async-start | bytes 3096576 | tf_op jit(solution)/shard_map/reduce_scatter | solution.py:53
  285.7 44.0 %slice-start.1 = ((s8[6291456]{0:T(1024)(128)(4,1)}), s8[4194304]{0:T(1024)(128)(4,1)S(1)}, s32[]{:S(2)}) async-start(s8[6291456]{0:T(1024)(128)(4,1)} %bitcast.68), calls=%async_computation.19 | async-start | bytes 8388608
  309.2 20.5 %copy-start.13 = (f32[4096]{0:T(1024)S(1)}, f32[4096]{0:T(1024)}, u32[]{:S(2)}) copy-start(f32[4096]{0:T(1024)} %copy-done.12) | copy-start | bytes 49156
  329.8 9.7 %copy-start.16 = (bf16[1,1792,768]{2,1,0:T(8,128)(2,1)S(1)}, bf16[1,1792,768]{2,1,0:T(8,128)(2,1)}, u32[]{:S(2)}) copy-start(bf16[1,1792,768]{2,1,0:T(8,128)(2,1)} %all-gather.17.cloned.1.call-done) | copy-start | bytes 8257540
  339.5 19.7 %copy-start.15 = (f32[4096]{0:T(1024)S(1)}, f32[4096]{0:T(1024)}, u32[]{:S(2)}) copy-start(f32[4096]{0:T(1024)} %copy-done.14) | copy-start | bytes 49156
  389.2 97.4 %reduce-scatter.13.cloned.1.call-start = ((), (), s32[]{:S(2)}) async-start(), calls=%async_computation.9 | async-start | bytes 3096576 | tf_op jit(solution)/shard_map/reduce_scatter | solution.py:53
  414.8 90.7 %reduce-scatter.11.cloned.1.call-start = ((), (), s32[]{:S(2)}) async-start(), calls=%async_computation.8 | async-start | bytes 3096576 | tf_op jit(solution)/shard_map/reduce_scatter | solution.py:53
  440.3 104.8 %reduce-scatter.17.cloned.1.call-start = ((), (), s32[]{:S(2)}) async-start(), calls=%async_computation.11 | async-start | bytes 3096576 | tf_op jit(solution)/shard_map/reduce_scatter | solution.py:53
  466.4 136.9 %copy-start.2 = (bf16[2,224,768]{2,1,0:T(8,128)(2,1)S(1)}, bf16[2,224,768]{2,1,0:T(8,128)(2,1)}, u32[]{:S(2)}) copy-start(bf16[2,224,768]{2,1,0:T(8,128)(2,1)} %param.15) | copy-start | bytes 2064388
  466.5 136.9 %copy-start.3 = (f32[2,224,768]{2,1,0:T(8,128)S(1)}, f32[2,224,768]{2,1,0:T(8,128)}, u32[]{:S(2)}) copy-start(f32[2,224,768]{2,1,0:T(8,128)} %param.21) | copy-start | bytes 4128772
  466.5 118.0 %reduce-scatter.15.cloned.1.call-start = ((), (), s32[]{:S(2)}) async-start(), calls=%async_computation.10 | async-start | bytes 3096576 | tf_op jit(solution)/shard_map/reduce_scatter | solution.py:53
  484.4 122.8 %copy-start = (bf16[2,96,1792]{2,1,0:T(8,128)(2,1)S(1)}, bf16[2,96,1792]{2,1,0:T(8,128)(2,1)}, u32[]{:S(2)}) copy-start(bf16[2,96,1792]{2,1,0:T(8,128)(2,1)} %param.13) | copy-start | bytes 2064388
  484.4 122.8 %copy-start.1 = (bf16[2,96,1792]{2,1,0:T(8,128)(2,1)S(1)}, bf16[2,96,1792]{2,1,0:T(8,128)(2,1)}, u32[]{:S(2)}) copy-start(bf16[2,96,1792]{2,1,0:T(8,128)(2,1)} %param.14) | copy-start | bytes 2064388
  603.3 3.9 copy-start.4
  603.4 3.9 copy-start.5
  603.4 3.9 copy-start.6
  603.4 3.9 copy-start.7
  603.4 3.9 copy-start.8
  603.4 4.2 copy-start.9
  603.4 4.6 copy-start.10
  603.4 4.7 copy-start.11
Sparse Core Ops, SparseCore 0:
  10.2 37.2 all-gather.12
  49.7 33.7 all-gather.14
  85.7 33.7 all-gather.16
  121.5 33.7 all-gather.22
  157.4 33.7 all-gather.20
  193.3 33.7 all-gather.18
  285.8 37.2 reduce-scatter.8
  389.3 37.3 reduce-scatter.6
  429.1 36.9 reduce-scatter.12
  468.3 37.1 reduce-scatter.10
  507.8 37.2 reduce-scatter.16
  547.2 37.1 reduce-scatter.14
where the time goes:
time: 626 us; the launch traced here: 619 us
  matrix products  357 us (57%)
  waiting for transfers between devices  176 us (28%)
  other arithmetic  27.5 us (4%)
  local copies, waits for them, and re-layouts  24.3 us (4%)
  between operations  17.3 us (3%)
  blocking collectives  15.5 us (2%)
    dot_general x5, matrix products, layer(): gate = jnp.dot(a, w['w_gate'], preferred_element_type=jnp.float32)  129 us
    dot_general x5, matrix products, layer(): up = jnp.dot(a, w['w_up'], preferred_element_type=jnp.float32)  128 us
    dot_general x5, matrix products, matmul(): jnp.dot(a, w, preferred_element_type=jnp.float32).astype(jnp.bfloat16)  100 us
    reduce_scatter x6, waiting for transfers between devices, step(): lax.psum_scatter(by_w[name], 'dp', scatter_dimension=0, tiled=True)  94.5 us
    all_gather x6, waiting for transfers between devices, fetched(): lax.all_gather(w[number], 'dp', axis=0, tiled=True)  80.1 us
    unnamed x40, local copies, waits for them, and re-layouts  18.4 us
    psum x1, blocking collectives, step(): squares = lax.psum(sum((jnp.sum(g * g) for g in gradients)), 'dp')  15.5 us
  transfers between devices with their start and end apart: 12, of which 9 were waited for; matrix products, arithmetic and copies ran while one was open for 55% of the time, Pallas kernels for 0%

commit v1 on v0

v1 whole, which is shorter than its diff:
```python
import functools

import jax
import jax.numpy as jnp
from jax import lax
from jax.experimental import pallas as pl
from jax.experimental.pallas import tpu as pltpu
from jax.sharding import PartitionSpec as P

LAYERS, TOKENS, D, FF = 2, 4096, 768, 1792
REPS, LINE, CORES = 4, 4, 2
GROUP = LINE * CORES
CHUNK = 256
CHUNKS = FF // CHUNK
LOCAL = CHUNK // GROUP
ROWS = D // GROUP
HALF = ROWS // 2
TILE = 512
TILES = TOKENS // TILE
ALL = LAYERS * CHUNKS
F32, BF16 = jnp.float32, jnp.bfloat16


def adamw(w, m, v, g):
    m = 0.9 * m + 0.1 * g
    v = 0.95 * v + 0.05 * g * g
    step = m * lax.rsqrt(v + 1e-8) + 0.1 * w
    return (w - 0.02 * step).astype(BF16), m, v


def dot(a, b, ca=1, cb=0):
    return lax.dot_general(a, b, (((ca,), (cb,)), ((), ())), preferred_element_type=F32)


def norm_scale(wide):
    return lax.rsqrt(jnp.mean(wide * wide, -1, keepdims=True) + 1e-6)


def kernel(
    x_hbm, dy_hbm, gu_hbm, d_hbm, ggu_out, gd_out, ss_out,
    abuf, xb, dyb, acc, wgu, wd, gg, gd,
    s1gu, s1d, r1gu, r1d, own_gu, own_d, sum_gu, sum_d, s2gu, s2d, r2gu, r2d, ssb,
    xsem, dysem, ownsem, a1send, a1recv, a2send, a2recv, a3send, a3recv,
    c1send, c1recv, c2send, c2recv, sssend, ssrecv,
):
    rep, me = lax.axis_index("rep"), lax.axis_index("dp")
    z, k = me // CORES, me % CORES
    other = 1 - k
    rg, rh = rep // 2, rep % 2

    barrier = pltpu.get_barrier_semaphore()
    for o in range(1, GROUP):
        pl.semaphore_signal(barrier, 1, device_id={"dp": (me + o) % GROUP})
    for o in range(1, REPS):
        pl.semaphore_signal(barrier, 1, device_id={"rep": (rep + o) % REPS})

    def tokens(t):
        return pl.ds(pl.multiple_of(t * TILE, TILE), TILE)

    def fetch(hbm, vmem, sem, t):
        return pltpu.make_async_copy(hbm.at[0, tokens(t)], vmem.at[tokens(t)], sem.at[t])

    for t in range(TILES):
        fetch(x_hbm, xb, xsem, t).start()
        fetch(dy_hbm, dyb, dysem, t).start()
    pl.semaphore_wait(barrier, GROUP - 1 + REPS - 1)

    def quarter(i):
        layer, c = i // CHUNKS, i % CHUNKS
        columns = pl.ds(pl.multiple_of(c * CHUNK, CHUNK), CHUNK)
        return (
            gu_hbm.at[layer, rg, rh, :, columns],
            d_hbm.at[layer, c, rg, :, pl.ds(pl.multiple_of(rh * (D // 2), D // 2), D // 2)],
        )

    def half_d(i):
        return wd.at[i, :, k, rg, :, pl.ds(pl.multiple_of(rh * (D // 2), D // 2), D // 2)]

    def gather1(i):
        gu, down = quarter(i)
        gu_to = wgu.at[i, rg, z, k, rh]
        d_to = wd.at[i, z, k, rg, :, pl.ds(pl.multiple_of(rh * (D // 2), D // 2), D // 2)]
        for o in range(1, LINE):
            to = {"dp": (z + o) % LINE * CORES + k}
            pltpu.make_async_remote_copy(gu, gu_to, a1send.at[0], a1recv.at[0, i], device_id=to).start()
            pltpu.make_async_remote_copy(down, d_to, a1send.at[1], a1recv.at[1, i], device_id=to).start()
        pltpu.make_async_copy(gu, gu_to, ownsem.at[0, i]).start()
        pltpu.make_async_copy(down, d_to, ownsem.at[1, i]).start()

    def wait_bytes(ref, sem):
        pltpu.make_async_copy(ref, ref, sem).wait()

    def gather2(i):
        wait_bytes(wgu.at[i, 0, pl.ds(0, LINE - 1), 0, 0], a1recv.at[0, i])
        wait_bytes(wd.at[i, pl.ds(0, LINE - 1), 0, 0, :, pl.ds(0, D // 2)], a1recv.at[1, i])
        wait_bytes(wgu.at[i, 0, 0, 0, 0], ownsem.at[0, i])
        wait_bytes(wd.at[i, 0, 0, 0, :, pl.ds(0, D // 2)], ownsem.at[1, i])
        gu, down = wgu.at[i, rg, :, k, rh], half_d(i)
        for o in range(1, REPS):
            to = {"rep": (rep + o) % REPS}
            pltpu.make_async_remote_copy(gu, gu, a2send.at[0], a2recv.at[0, i], device_id=to).start()
            pltpu.make_async_remote_copy(down, down, a2send.at[1], a2recv.at[1, i], device_id=to).start()

    def gather3(i):
        wait_bytes(wgu.at[i, 0, pl.ds(0, REPS - 1)], a2recv.at[0, i])
        wait_bytes(wd.at[i, pl.ds(0, REPS - 1), :, 0], a2recv.at[1, i])
        gu, down = wgu.at[i, :, :, k], wd.at[i, :, k]
        to = {"dp": z * CORES + other}
        pltpu.make_async_remote_copy(gu, gu, a3send.at[0], a3recv.at[0, i], device_id=to).start()
        pltpu.make_async_remote_copy(down, down, a3send.at[1], a3recv.at[1, i], device_id=to).start()

    def arrived(i):
        wait_bytes(wgu.at[i, :, :, 0], a3recv.at[0, i])
        wait_bytes(wd.at[i, :, 0], a3recv.at[1, i])

    def gathered(i):
        pl.when(i + 2 < ALL)(lambda: gather2(i + 2))
        pl.when(i + 1 < ALL)(lambda: gather3(i + 1))
        arrived(i)

    pl.loop(0, ALL)(gather1)
    acc[...] = jnp.zeros_like(acc)

    @pl.loop(0, TILES)
    def _(t):
        fetch(x_hbm, xb, xsem, t).wait()
        wide = xb[tokens(t)].astype(F32)
        abuf[tokens(t)] = (wide * norm_scale(wide)).astype(BF16)

    gather2(0)
    gather2(1)
    gather3(0)

    def weights(i):
        gu = wgu[i]
        return gu[0].reshape(D, CHUNK), gu[1].reshape(D, CHUNK), wd[i].reshape(CHUNK, D)

    @pl.loop(0, CHUNKS)
    def _(c):
        gathered(c)

        @pl.loop(0, TILES)
        def _(t):
            wg, wu, down = weights(c)
            a = abuf[tokens(t)]
            gate, up = dot(a, wg), dot(a, wu)
            hidden = (gate * jax.nn.sigmoid(gate) * up).astype(BF16)
            acc[tokens(t)] += dot(hidden, down)

    @pl.loop(0, TILES)
    def _(t):
        h = xb[tokens(t)] + acc[tokens(t)].astype(BF16)
        xb[tokens(t)] = h
        wide = h.astype(F32)
        abuf[tokens(t)] = (wide * norm_scale(wide)).astype(BF16)
        acc[tokens(t)] = jnp.zeros((TILE, D), F32)
        fetch(dy_hbm, dyb, dysem, t).wait()

    def backward(i, t, first, with_input):
        wg, wu, down = weights(i)
        a, by_y = abuf[tokens(t)], dyb[tokens(t)]
        gate, up = dot(a, wg), dot(a, wu)
        by_hidden = dot(by_y, down, 1, 1).astype(BF16).astype(F32)
        s = jax.nn.sigmoid(gate)
        silu = gate * s
        hidden = (silu * up).astype(BF16)
        by_up = (by_hidden * silu).astype(BF16)
        by_gate = (by_hidden * up * (s + silu * (1.0 - s))).astype(BF16)

        def add(ref, value):
            ref[...] = value.reshape(ref.shape) if first else ref[...] + value.reshape(ref.shape)

        add(gd, dot(hidden, by_y, 0, 0))
        add(gg.at[0], dot(a, by_gate, 0, 0))
        add(gg.at[1], dot(a, by_up, 0, 0))
        if with_input:
            acc[tokens(t)] += dot(by_gate, wg, 1, 1) + dot(by_up, wu, 1, 1)

    def partner_copies(q):
        to, s = {"dp": z * CORES + other}, q % 2
        return (
            pltpu.make_async_remote_copy(s1gu, r1gu.at[s], c1send.at[0], c1recv.at[0, s], device_id=to),
            pltpu.make_async_remote_copy(s1d, r1d.at[s], c1send.at[1], c1recv.at[1, s], device_id=to),
        )

    def scatter1(q):
        s1gu[...] = gg[:, :, other].astype(BF16)
        s1d[...] = gd[:, other].astype(BF16)
        for copy in partner_copies(q):
            copy.start()
        own_gu[...] = gg[:, :, k]
        own_d[...] = gd[:, k]

    def wait_line_sends(s):
        wait_bytes(s2gu.at[s, pl.ds(0, LINE - 1)], c2send.at[0, s])
        wait_bytes(s2d.at[s, pl.ds(0, LINE - 1)], c2send.at[1, s])

    def scatter2(q):
        s = q % 2
        for copy in partner_copies(q):
            copy.wait()
        pl.when(q >= 2)(lambda: wait_line_sends(s))
        pair_gu = own_gu[...] + r1gu[s].astype(F32)
        pair_d = own_d[...] + r1d[s].astype(F32)
        for g in range(2):
            s2gu[s, :, g] = pair_gu[g].astype(BF16)
        s2d[s] = pair_d.astype(BF16)
        own_gu[...] = pair_gu
        own_d[...] = pair_d
        sum_gu[s] = own_gu[:, z]
        sum_d[s] = own_d[z]
        for o in range(1, LINE):
            there = (z + o) % LINE
            to = {"dp": there * CORES + k}
            pltpu.make_async_remote_copy(s2gu.at[s, there], r2gu.at[s, o - 1], c2send.at[0, s], c2recv.at[0, s, o - 1], device_id=to).start()
            pltpu.make_async_remote_copy(s2d.at[s, there], r2d.at[s, o - 1], c2send.at[1, s], c2recv.at[1, s, o - 1], device_id=to).start()

    def scatter3(q):
        s = q % 2
        for o in range(LINE - 1):
            wait_bytes(r2gu.at[s, o], c2recv.at[0, s, o])
            wait_bytes(r2d.at[s, o], c2recv.at[1, s, o])
        total_gu, total_d = sum_gu[s], sum_d[s]
        for o in range(LINE - 1):
            total_gu += r2gu[s, o].astype(F32)
            total_d += r2d[s, o].astype(F32)
        total_gu, total_d = total_gu.astype(BF16), total_d.astype(BF16)
        layer, c = LAYERS - 1 - q // CHUNKS, q % CHUNKS
        for g in range(2):
            ggu_out[layer, g, :, pl.ds(pl.multiple_of(c * CHUNK, CHUNK), CHUNK)] = total_gu[g]
        gd_out[layer, c] = total_d
        wide_gu, wide_d = total_gu.astype(F32), total_d.astype(F32)
        squares = (wide_gu * wide_gu).reshape(2, ROWS // 8, 8, CHUNK).sum((0, 1))
        squares_d = (wide_d * wide_d).reshape(LOCAL // 8, 8, D).sum(0)
        ssb[0] += sum(squares[:, n : n + 128] for n in range(0, CHUNK, 128)) + sum(squares_d[:, n : n + 128] for n in range(0, D, 128))

    ssb[0] = jnp.zeros((8, 128), F32)

    def layer_backward(base, q0, with_input, weights_come):
        @pl.loop(0, CHUNKS)
        def _(c):
            i, q = base + c, q0 + c
            if weights_come:
                gathered(i)
            backward(i, 0, True, with_input)
            pl.when(q >= 2)(lambda: scatter3(q - 2))
            pl.when(q >= 1)(lambda: scatter2(q - 1))

            @pl.loop(1, TILES)
            def _(t):
                backward(i, t, False, with_input)

            scatter1(q)

    layer_backward(CHUNKS, 0, True, True)

    @pl.loop(0, TILES)
    def _(t):
        wide = xb[tokens(t)].astype(F32)
        by_a = acc[tokens(t)].astype(BF16).astype(F32)
        scale = norm_scale(wide)
        inner = jnp.mean(wide * by_a, -1, keepdims=True)
        by_h = by_a * scale - wide * (scale * scale * scale * inner)
        dyb[tokens(t)] = dyb[tokens(t)] + by_h.astype(BF16)
        fetch(x_hbm, xb, xsem, t).start()

    @pl.loop(0, TILES)
    def _(t):
        fetch(x_hbm, xb, xsem, t).wait()
        wide = xb[tokens(t)].astype(F32)
        abuf[tokens(t)] = (wide * norm_scale(wide)).astype(BF16)

    layer_backward(0, CHUNKS, False, False)
    scatter3(ALL - 2)
    scatter2(ALL - 1)
    scatter3(ALL - 1)

    def square_copy(o):
        return pltpu.make_async_remote_copy(ssb.at[0], ssb.at[o], sssend.at[o - 1], ssrecv.at[o - 1], device_id={"dp": (me + o) % GROUP})

    for o in range(1, GROUP):
        square_copy(o).start()
    for o in range(1, GROUP):
        square_copy(o).wait()
    ss_out[...] = sum(ssb[o] for o in range(GROUP))

    for s in range(2):
        wait_line_sends(s)
    wait_bytes(wgu.at[:, 0, pl.ds(0, LINE - 1), 0, 0], a1send.at[0])
    wait_bytes(wd.at[:, pl.ds(0, LINE - 1), 0, 0, :, pl.ds(0, D // 2)], a1send.at[1])
    wait_bytes(wgu.at[:, 0, pl.ds(0, REPS - 1)], a2send.at[0])
    wait_bytes(wd.at[:, pl.ds(0, REPS - 1), :, 0], a2send.at[1])
    wait_bytes(wgu.at[:, :, :, 0], a3send.at[0])
    wait_bytes(wd.at[:, :, 0], a3send.at[1])


def gradients(x, dy, gu, down):
    vm, dma = pltpu.VMEM, pltpu.SemaphoreType.DMA
    flops = 17 * 2 * TOKENS * D * FF
    return pl.pallas_call(
        kernel,
        out_shape=(
            jax.ShapeDtypeStruct((LAYERS, 2, ROWS, FF), BF16),
            jax.ShapeDtypeStruct((LAYERS, CHUNKS, LOCAL, D), BF16),
            jax.ShapeDtypeStruct((8, 128), F32),
        ),
        in_specs=[pl.BlockSpec(memory_space=pl.ANY)] * 4,
        out_specs=(pl.BlockSpec(memory_space=pltpu.VMEM),) * 3,
        scratch_shapes=[
            vm((TOKENS, D), BF16), vm((TOKENS, D), BF16), vm((TOKENS, D), BF16), vm((TOKENS, D), F32),
            vm((ALL, 2, LINE, CORES, 2, HALF, CHUNK), BF16), vm((ALL, LINE, CORES, 2, LOCAL // 2, D), BF16),
            vm((2, LINE, CORES, ROWS, CHUNK), F32), vm((LINE, CORES, LOCAL, D), F32),
            vm((2, LINE, ROWS, CHUNK), BF16), vm((LINE, LOCAL, D), BF16),
            vm((2, 2, LINE, ROWS, CHUNK), BF16), vm((2, LINE, LOCAL, D), BF16),
            vm((2, LINE, ROWS, CHUNK), F32), vm((LINE, LOCAL, D), F32),
            vm((2, 2, ROWS, CHUNK), F32), vm((2, LOCAL, D), F32),
            vm((2, LINE, 2, ROWS, CHUNK), BF16), vm((2, LINE, LOCAL, D), BF16),
            vm((2, LINE - 1, 2, ROWS, CHUNK), BF16), vm((2, LINE - 1, LOCAL, D), BF16),
            vm((GROUP, 8, 128), F32),
            dma((TILES,)), dma((TILES,)), dma((2, ALL)), dma((2,)), dma((2, ALL)), dma((2,)), dma((2, ALL)), dma((2,)), dma((2, ALL)),
            dma((2,)), dma((2, 2)), dma((2, 2)), dma((2, 2, LINE - 1)), dma((GROUP - 1,)), dma((GROUP - 1,)),
        ],
        compiler_params=pltpu.CompilerParams(collective_id=0, has_side_effects=True, vmem_limit_bytes=67043328),
        cost_estimate=pl.CostEstimate(flops=flops, bytes_accessed=2 * TOKENS * D * 2, transcendentals=0),
    )(x, dy, gu, down)


def solution(mesh):
    def step(x, dy, w_gate, w_up, w_down, m_gate, m_up, m_down, v_gate, v_up, v_down):
        at = lax.broadcasted_iota(jnp.int32, (FF, FF), 0)
        to = lax.broadcasted_iota(jnp.int32, (FF, FF), 1)
        own = (to % CHUNK) // LOCAL * (FF // GROUP) + to // CHUNK * LOCAL + to % LOCAL
        order = (at == own).astype(BF16)
        gu = jnp.stack([w_gate, w_up], 1)
        placed = jnp.dot(gu.reshape(-1, FF), order, preferred_element_type=F32).astype(BF16)
        ggu, gd, squares = gradients(
            x, dy, placed.reshape(LAYERS, 2, 2, HALF, FF), w_down.reshape(LAYERS, CHUNKS, 2, LOCAL // 2, D)
        )
        ggu = lax.dot_general(ggu.reshape(-1, FF), order, (((1,), (1,)), ((), ())), preferred_element_type=F32).reshape(LAYERS, 2, ROWS, FF)
        g = [ggu[:, 0], ggu[:, 1], gd.reshape(w_down.shape).astype(F32)]
        count = GROUP * sum(one.size for one in g)
        factor = jnp.minimum(1.0, 0.5 * lax.rsqrt(jnp.sum(squares) / count + 1e-30))
        new = [
            adamw(w.astype(F32), m, v, one * factor)
            for w, m, v, one in zip((w_gate, w_up, w_down), (m_gate, m_up, m_down), (v_gate, v_up, v_down), g, strict=True)
        ]
        return tuple(one[which] for which in range(3) for one in new)

    states, cut = P(("rep", "dp"), None, None), P(None, "dp", None)
    return jax.shard_map(
        step,
        mesh=mesh,
        in_specs=(states, states) + (cut,) * 9,
        out_specs=(P("rep", "dp", None),) * 9,
        check_vma=False,
    )
```

time: 626 us -> 344 us (0.55); the launches traced: 619 us -> 344 us
  matrix products: 357 us -> 10.4 us
  Pallas kernels: 0 us -> 320 us
  waiting for transfers between devices: 176 us -> 0 us
  local copies, waits for them, and re-layouts: 24.3 us -> 1.44 us
  other arithmetic: 27.5 us -> 11.1 us
  between operations: 17.3 us -> 1.62 us
  blocking collectives: 15.5 us -> 0 us
    dot_general x15 -> x2, matrix products: 357 us -> 10.4 us  [the longest x1 6.13 us: step(): lax.dot_general(ggu.reshape(-1, FF), order, (((1,), (1,)), ((), ())), pre...]
    pallas_call x0 -> x1, Pallas kernels: none -> 320 us  [gradients(): pl.pallas_call(kernel, out_shape=(jax.ShapeDtypeStruct((LAYERS, 2, ROWS,...]
    reduce_scatter x6 -> x0, waiting for transfers between devices: 94.5 us -> none  [step(): lax.psum_scatter(by_w[name], 'dp', scatter_dimension=0, tiled=True)]
    all_gather x6 -> x0, waiting for transfers between devices: 80.1 us -> none  [fetched(): lax.all_gather(w[number], 'dp', axis=0, tiled=True)]
    unnamed x40 -> x34, local copies, waits for them, and re-layouts: 18.4 us -> 1.44 us
    psum x1 -> x0, blocking collectives: 15.5 us -> none  [step(): squares = lax.psum(sum((jnp.sum(g * g) for g in gradients)), 'dp')]
    reduce_sum x4 -> x1, other arithmetic: 10.3 us -> 0.6 us  [step(): factor = jnp.minimum(1.0, 0.5 * lax.rsqrt(jnp.sum(squares) / count + 1e-30))]
    add_any x1 -> x0, other arithmetic: 9.67 us -> none  [normed(): wide = h.astype(jnp.float32)]
  transfers between devices with their start and end apart: 12 -> 0, of which waited for: 9 -> 0; matrix products, arithmetic and copies ran while one was open for 55% -> 0% of each run, Pallas kernels for 0% -> 0%
where the time goes in v1:
time: 344 us
  Pallas kernels  320 us (93%)
  other arithmetic  11.1 us (3%)
  matrix products  10.4 us (3%)
    pallas_call x1, Pallas kernels, gradients(): pl.pallas_call(kernel, out_shape=(jax.ShapeDtypeStruct((LAYERS, 2, ROWS,...  320 us
    convert_element_type x2, other arithmetic, adamw(): return ((w - 0.02 * step).astype(BF16), m, v)  8.86 us

profile of v1, /device:TPU:0, one launch (start us, length us, event | category | flops | bytes accessed | tf_op | source)
XLA Modules:
  0.0 344.1 jit_solution(13103226445141681770)
XLA Ops:
  0.7 0.0 copy-start.7
  0.7 0.0 copy-start.8
  0.7 0.0 copy-start.9
  0.7 0.0 copy-start.10
  0.7 0.0 copy-start.11
  0.7 0.0 copy-start.12
  0.8 0.0 copy-start.14
  0.8 0.0 copy-start.15
  0.8 0.0 copy-start.16
  0.8 1.4 pad_maximum_fusion
  2.2 0.0 copy-done.7
  2.3 0.0 copy-done.8
  2.3 0.0 copy-done.9
  2.3 0.0 copy-done.10
  2.3 0.0 copy-done.11
  2.3 0.0 copy-done.12
  2.3 0.0 copy-done.14
  2.3 0.0 copy-done.15
  2.3 0.0 copy-done.16
  2.3 4.3 %convolution_convert_fusion = bf16[384,1792]{1,0:T(8,128)(2,1)} fusion(bf16[384,1792]{1,0:T(8,128)(2,1)S(1)} %bitcast.57, s32[1792]{0:T(1024)S(1)} %get-tuple-element.27, s32[1792]{0:T(1024)S(1)} %get-tuple-element.31, s32[1792]{0:T(1024)S(1)} %get-tuple-element.28, s32[1792]{0:T(1024)S(1)} %get-tuple-element.32, s32[1792]{0:T(1024)S(1)} %get-tuple-element.29, ...), kind=kOutput, calls=%fused_computation.18 | convolution fusion | flops 2540797952 | bytes 2800896 | tf_op jit(solution)/shard_map/dot_general | solution.py:335
  6.6 319.6 %shard_map.178 = (bf16[2,2,96,1792]{3,2,1,0:T(8,128)(2,1)}, bf16[2,7,32,768]{3,2,1,0:T(8,128)(2,1)}, f32[8,128]{1,0:T(8,128)}) custom-call(bf16[1,4096,768]{2,1,0:T(8,128)(2,1)} %x_hbm.1, bf16[1,4096,768]{2,1,0:T(8,128)(2,1)} %dy_hbm.1, bf16[2,2,2,48,1792]{4,3,2,1,0:T(8,128)(2,1)} %bitcast.59, bf16[2,7,2,16,768]{4,3,2,1,0:T(8,128)(2,1)} %bitcast.58), custom_call_target="tpu_custom_call" | custom-call | flops 191662915584 | bytes 12582912 | tf_op jit(solution)/shard_map/pallas_call | solution.py:300
  326.2 0.0 copy-start.13
  326.2 0.0 copy-start
  326.2 0.0 copy-start.1
  326.2 0.0 copy-start.2
  326.2 6.1 %fusion.9 = f32[2,2,96,1792]{3,2,1,0:T(8,128)} fusion(bf16[2,2,96,1792]{3,2,1,0:T(8,128)(2,1)} %get-tuple-element.12, s32[1792]{0:T(1024)} %copy-done.7, s32[1792]{0:T(1024)} %copy-done.11, s32[1792]{0:T(1024)} %copy-done.8, s32[1792]{0:T(1024)} %copy-done.12, s32[1792]{0:T(1024)} %copy-done.9, s32[1792]{0:T(1024)} %copy-done.10, ...), kind=kOutput, calls=%fused_computation.16 | convolution fusion | flops 2540109824 | bytes 4177152 | tf_op jit(solution)/shard_map/dot_general | solution.py:339
  332.4 0.0 copy-done.13
  332.4 0.6 reduce_sum.9
  333.7 0.0 copy-done
  333.7 0.0 copy-done.1
  333.7 0.0 copy-done.2
  333.7 0.0 copy-start.5
  333.7 0.0 copy-start.4
  333.7 6.8 %fusion.16 = (bf16[2,96,1792]{2,1,0:T(8,128)(2,1)}, f32[2,96,1792]{2,1,0:T(8,128)}, f32[2,96,1792]{2,1,0:T(8,128)}, bf16[2,96,1792]{2,1,0:T(8,128)(2,1)}, f32[2,96,1792]{2,1,0:T(8,128)}, /*index=5*/f32[2,96,1792]{2,1,0:T(8,128)}) fusion(bf16[2,96,1792]{2,1,0:T(8,128)(2,1)S(1)} %copy-done, f32[]{:T(128)S(6)} %min_shard_map.3, f32[2,2,96,1792]{3,2,1,0:T(8,128)} %fusion.9, ...), kind=kLoop, calls=%fused_computation.33 | loop fusion | flops 11010048 | bytes 16515076 | tf_op jit(solution)/shard_map/convert_element_type | solution.py:28
  340.5 0.0 copy-start.3
  340.5 0.0 copy-start.6
  340.5 0.0 copy-done.5
  340.5 0.1 convert_multiply_fusion.3
  340.6 0.0 copy-done.4
  340.6 1.2 copy-done.3
  341.8 0.2 copy-done.6
  342.0 2.1 fusion.19
  (5 shorter events, 0.0 us)
Async XLA Ops:
  0.7 1.6 copy-start.7
  0.7 1.6 copy-start.8
  0.7 1.6 copy-start.9
  0.7 1.6 copy-start.10
  0.7 1.6 copy-start.11
  0.7 1.6 copy-start.12
  0.8 1.6 copy-start.14
  0.8 1.5 copy-start.15
  0.8 1.5 copy-start.16
  326.2 6.2 %copy-start.13 = (f32[8,128]{1,0:T(8,128)S(1)}, f32[8,128]{1,0:T(8,128)}, u32[]{:S(2)}) copy-start(f32[8,128]{1,0:T(8,128)} %get-tuple-element.13) | copy-start | bytes 12292
  326.2 7.5 %copy-start = (bf16[2,96,1792]{2,1,0:T(8,128)(2,1)S(1)}, bf16[2,96,1792]{2,1,0:T(8,128)(2,1)}, u32[]{:S(2)}) copy-start(bf16[2,96,1792]{2,1,0:T(8,128)(2,1)} %param.14) | copy-start | bytes 2064388
  326.2 7.5 %copy-start.1 = (bf16[2,96,1792]{2,1,0:T(8,128)(2,1)S(1)}, bf16[2,96,1792]{2,1,0:T(8,128)(2,1)}, u32[]{:S(2)}) copy-start(bf16[2,96,1792]{2,1,0:T(8,128)(2,1)} %param.13) | copy-start | bytes 2064388
  326.2 7.5 %copy-start.2 = (f32[2,96,1792]{2,1,0:T(8,128)S(1)}, f32[2,96,1792]{2,1,0:T(8,128)}, u32[]{:S(2)}) copy-start(f32[2,96,1792]{2,1,0:T(8,128)} %param.20) | copy-start | bytes 4128772
  333.7 6.8 %copy-start.5 = (bf16[2,7,32,768]{3,2,1,0:T(8,128)(2,1)S(1)}, bf16[2,7,32,768]{3,2,1,0:T(8,128)(2,1)}, u32[]{:S(2)}) copy-start(bf16[2,7,32,768]{3,2,1,0:T(8,128)(2,1)} %get-tuple-element.14) | copy-start | bytes 2064388
  333.7 6.9 %copy-start.4 = (f32[2,224,768]{2,1,0:T(8,128)S(1)}, f32[2,224,768]{2,1,0:T(8,128)}, u32[]{:S(2)}) copy-start(f32[2,224,768]{2,1,0:T(8,128)} %param.18) | copy-start | bytes 4128772
  340.5 1.3 copy-start.3
  340.5 1.5 copy-start.6

commit v2 on v1

v2 whole, which is shorter than its diff:
```python
import functools

import jax
import jax.numpy as jnp
import numpy as np
from jax import lax
from jax.experimental import pallas as pl
from jax.experimental.pallas import tpu as pltpu
from jax.sharding import PartitionSpec as P

LAYERS, TOKENS, D, FF = 2, 4096, 768, 1792
REPS, LINE, CORES = 4, 4, 2
GROUP = LINE * CORES
CHUNK = 256
CHUNKS = FF // CHUNK
LOCAL = CHUNK // GROUP
ROWS = D // GROUP
HALF = ROWS // 2
TILE = 1024
TILES = TOKENS // TILE
AHEAD = 4
SLOTS = 3
ALL = LAYERS * CHUNKS
F32, BF16 = jnp.float32, jnp.bfloat16
ORDER = np.arange(FF, dtype=np.int32).reshape(GROUP, CHUNKS, LOCAL).transpose(1, 0, 2).reshape(FF)


def adamw(w, m, v, g):
    m = 0.9 * m + 0.1 * g
    v = 0.95 * v + 0.05 * g * g
    step = m * lax.rsqrt(v + 1e-8) + 0.1 * w
    return (w - 0.02 * step).astype(BF16), m, v


def dot(a, b, ca=1, cb=0):
    return lax.dot_general(a, b, (((ca,), (cb,)), ((), ())), preferred_element_type=F32)


def norm_scale(wide):
    return lax.rsqrt(jnp.mean(wide * wide, -1, keepdims=True) + 1e-6)


def kernel(
    x_hbm, dy_hbm, gu_hbm, d_hbm, ggu_out, gd_out, ss_out,
    abuf, xb, dyb, acc, wgu, wd, gg, gd,
    s1gu, s1d, r1gu, r1d, sum_gu, sum_d, s2gu, s2d, r2gu, r2d, sogu, sod, rogu, rod, sumogu, sumod, s3gu, s3d, r3gu, r3d, ssb,
    xsem, dysem, ownsem, a1send, a1recv, a2send, a2recv, a3send, a3recv,
    c1send, c1recv, c2send, c2recv, cosend, corecv, c3send, c3recv, mate_free, across_free, sssend, ssrecv,
):
    rep, me = lax.axis_index("rep"), lax.axis_index("dp")
    z, k = me // CORES, me % CORES
    other = 1 - k
    rg, rh = rep // 2, rep % 2

    barrier = pltpu.get_barrier_semaphore()
    for o in range(1, GROUP):
        pl.semaphore_signal(barrier, 1, device_id={"dp": (me + o) % GROUP})
    for o in range(1, REPS):
        pl.semaphore_signal(barrier, 1, device_id={"rep": (rep + o) % REPS})

    def tokens(t):
        return pl.ds(pl.multiple_of(t * TILE, TILE), TILE)

    def fetch(hbm, vmem, sem, t):
        return pltpu.make_async_copy(hbm.at[0, tokens(t)], vmem.at[tokens(t)], sem.at[t])

    for t in range(TILES):
        fetch(x_hbm, xb, xsem, t).start()
        fetch(dy_hbm, dyb, dysem, t).start()
    pl.semaphore_wait(barrier, GROUP - 1 + REPS - 1)

    def wait_bytes(ref, sem):
        pltpu.make_async_copy(ref, ref, sem).wait()

    d_half = pl.ds(pl.multiple_of(rh * (D // 2), D // 2), D // 2)

    def quarter(i, line):
        return wgu.at[i, rg, line, k, rh], wd.at[i, line, k, rg, :, d_half]

    def gather1(i):
        layer, c = i // CHUNKS, i % CHUNKS
        columns = pl.ds(pl.multiple_of(c * CHUNK, CHUNK), CHUNK)
        gu, down = gu_hbm.at[layer, rg, rh, :, columns], d_hbm.at[layer, c, rg, :, d_half]
        gu_to, d_to = quarter(i, z)
        for o in range(1, LINE):
            to = {"dp": (z + o) % LINE * CORES + k}
            pltpu.make_async_remote_copy(gu, gu_to, a1send.at[0], a1recv.at[0, i], device_id=to).start()
            pltpu.make_async_remote_copy(down, d_to, a1send.at[1], a1recv.at[1, i], device_id=to).start()
        pltpu.make_async_copy(gu_hbm.at[layer, :, :, :, columns], wgu.at[i, :, z, k], ownsem.at[0, i]).start()
        pltpu.make_async_copy(d_hbm.at[layer, c], wd.at[i, z, k], ownsem.at[1, i]).start()

    def gather2(i):
        wait_bytes(wgu.at[i, 0, pl.ds(0, LINE - 1), 0, 0], a1recv.at[0, i])
        wait_bytes(wd.at[i, pl.ds(0, LINE - 1), 0, 0, :, pl.ds(0, D // 2)], a1recv.at[1, i])
        for o in range(1, LINE):
            gu, down = quarter(i, (z + o) % LINE)
            for p in range(1, REPS):
                to = {"rep": (rep + p) % REPS}
                pltpu.make_async_remote_copy(gu, gu, a2send.at[0], a2recv.at[0, i], device_id=to).start()
                pltpu.make_async_remote_copy(down, down, a2send.at[1], a2recv.at[1, i], device_id=to).start()

    def gather3(i):
        wait_bytes(wgu.at[pl.ds(0, REPS - 1), 0, pl.ds(0, LINE - 1), 0, 0], a2recv.at[0, i])
        wait_bytes(wd.at[pl.ds(0, REPS - 1), pl.ds(0, LINE - 1), 0, 0, :, pl.ds(0, D // 2)], a2recv.at[1, i])
        wait_bytes(wgu.at[i, :, 0, 0], ownsem.at[0, i])
        wait_bytes(wd.at[i, 0, 0], ownsem.at[1, i])
        gu, down = wgu.at[i, :, :, k], wd.at[i, :, k]
        to = {"dp": z * CORES + other}
        pltpu.make_async_remote_copy(gu, gu, a3send.at[0], a3recv.at[0, i], device_id=to).start()
        pltpu.make_async_remote_copy(down, down, a3send.at[1], a3recv.at[1, i], device_id=to).start()

    def arrived(i):
        wait_bytes(wgu.at[i, :, :, 0], a3recv.at[0, i])
        wait_bytes(wd.at[i, :, 0], a3recv.at[1, i])

    def gather_on(i, t):
        pl.when((t == 1) & (i + AHEAD < ALL))(lambda: gather1(i + AHEAD))
        pl.when((t == 1) & (i + 2 < ALL))(lambda: gather2(i + 2))
        pl.when((t == 2) & (i + 1 < ALL))(lambda: gather3(i + 1))

    pl.loop(0, AHEAD)(gather1)
    acc[...] = jnp.zeros_like(acc)

    @pl.loop(0, TILES)
    def _(t):
        fetch(x_hbm, xb, xsem, t).wait()
        wide = xb[tokens(t)].astype(F32)
        abuf[tokens(t)] = (wide * norm_scale(wide)).astype(BF16)

    gather2(0)
    gather2(1)
    gather3(0)

    def weights(i):
        gu = wgu[i]
        return gu[0].reshape(D, CHUNK), gu[1].reshape(D, CHUNK), wd[i].reshape(CHUNK, D)

    @pl.loop(0, CHUNKS)
    def _(c):
        arrived(c)

        @pl.loop(0, TILES)
        def _(t):
            gather_on(c, t)
            wg, wu, down = weights(c)
            a = abuf[tokens(t)]
            gate, up = dot(a, wg), dot(a, wu)
            hidden = (gate * jax.nn.sigmoid(gate) * up).astype(BF16)
            acc[tokens(t)] += dot(hidden, down)

    @pl.loop(0, TILES)
    def _(t):
        h = xb[tokens(t)] + acc[tokens(t)].astype(BF16)
        xb[tokens(t)] = h
        wide = h.astype(F32)
        abuf[tokens(t)] = (wide * norm_scale(wide)).astype(BF16)
        acc[tokens(t)] = jnp.zeros((TILE, D), F32)
        fetch(dy_hbm, dyb, dysem, t).wait()

    def backward(i, t, s, with_input):
        wg, wu, down = weights(i)
        a, by_y = abuf[tokens(t)], dyb[tokens(t)]
        gate, up = dot(a, wg), dot(a, wu)
        by_hidden = dot(by_y, down, 1, 1).astype(BF16).astype(F32)
        sig = jax.nn.sigmoid(gate)
        silu = gate * sig
        hidden = (silu * up).astype(BF16)
        by_up = (by_hidden * silu).astype(BF16)
        by_gate = (by_hidden * up * (sig + silu * (1.0 - sig))).astype(BF16)

        def add(ref, value):
            ref[...] = jnp.where(t == 0, 0.0, ref[...]) + value.reshape(ref.shape)

        add(gd.at[s], dot(hidden, by_y, 0, 0))
        add(gg.at[s, 0], dot(a, by_gate, 0, 0))
        add(gg.at[s, 1], dot(a, by_up, 0, 0))
        if with_input:
            acc[tokens(t)] += dot(by_gate, wg, 1, 1) + dot(by_up, wu, 1, 1)

    def partner_copies(q):
        to, s = {"dp": z * CORES + other}, q % 2
        return (
            pltpu.make_async_remote_copy(s1gu, r1gu.at[s], c1send.at[0], c1recv.at[0, s], device_id=to),
            pltpu.make_async_remote_copy(s1d, r1d.at[s], c1send.at[1], c1recv.at[1, s], device_id=to),
        )

    def scatter1(q):
        s1gu[...] = gg[q % 2, :, :, other].astype(BF16)
        s1d[...] = gd[q % 2, :, other].astype(BF16)
        for copy in partner_copies(q):
            copy.start()

    mate, side = z + 1 - 2 * (z % 2), z // 2
    across = (LINE // 2) * (1 - side)
    middle = (z + 1) // 2 % 2 == 1

    def mate_copies(q):
        to, s, r = {"dp": mate * CORES + k}, q % 2, q % SLOTS
        return (
            pltpu.make_async_remote_copy(s2d.at[s], r2d.at[r], c2send.at[0, s], c2recv.at[0, r], device_id=to),
            pltpu.make_async_remote_copy(s2gu.at[s], r2gu.at[r], c2send.at[1, s], c2recv.at[1, r], device_id=to),
        )

    def end_copies(q):
        to, s, r = {"dp": mate * CORES + k}, q % 2, q % SLOTS
        return (
            pltpu.make_async_remote_copy(sod.at[s], rod.at[r], cosend.at[0, s], corecv.at[0, r], device_id=to),
            pltpu.make_async_remote_copy(sogu.at[s], rogu.at[r], cosend.at[1, s], corecv.at[1, r], device_id=to),
        )

    def scatter2(q):
        s = q % 2
        for copy in partner_copies(q):
            copy.wait()

        @pl.when(q >= 2)
        def _():
            for copy in mate_copies(q):
                copy.wait_send()

            @pl.when(jnp.logical_not(middle))
            def _():
                for copy in end_copies(q):
                    copy.wait_send()

        pl.when(q >= SLOTS)(lambda: pl.semaphore_wait(mate_free, 1))
        two = pl.ds(across, LINE // 2)

        @pl.when(jnp.logical_not(middle))
        def _():
            sod[s] = (gd[s, two, k] + r1d[s, two].astype(F32)).astype(BF16)
            for g in range(2):
                sogu[s, g] = (gg[s, g, two, k] + r1gu[s, g, two].astype(F32)).astype(BF16)
            for copy in end_copies(q):
                copy.start()

        @pl.when(middle)
        def _():
            sumod[...] = gd[s, two, k] + r1d[s, two].astype(F32)
            for g in range(2):
                sumogu[g] = gg[s, g, two, k] + r1gu[s, g, two].astype(F32)

        s2d[s] = (gd[s, mate, k] + r1d[s, mate].astype(F32)).astype(BF16)
        for g in range(2):
            s2gu[s, g] = (gg[s, g, mate, k] + r1gu[s, g, mate].astype(F32)).astype(BF16)
        for copy in mate_copies(q):
            copy.start()
        sum_d[s] = gd[s, z, k] + r1d[s, z].astype(F32)
        for g in range(2):
            sum_gu[s, g] = gg[s, g, z, k] + r1gu[s, g, z].astype(F32)

    def across_copies(q, array):
        s, r = q % 2, q % SLOTS
        to = [{"dp": (across + u) * CORES + k} for u in range(2)]
        if array == 0:
            return [pltpu.make_async_remote_copy(s3d.at[s, u], r3d.at[r], c3send.at[0, s, u], c3recv.at[0, r], device_id=to[u]) for u in range(2)]
        return [pltpu.make_async_remote_copy(s3gu.at[s, u], r3gu.at[r], c3send.at[1, s, u], c3recv.at[1, r], device_id=to[u]) for u in range(2)]

    def scatter3(q):
        @pl.when(middle)
        def _():
            s, r = q % 2, q % SLOTS

            @pl.when(q >= 2)
            def _():
                for copy in across_copies(q, 0) + across_copies(q, 1):
                    copy.wait_send()

            @pl.when(q >= SLOTS)
            def _():
                for u in range(2):
                    pl.semaphore_wait(across_free.at[u], 1)

            wait_bytes(rod.at[r], corecv.at[0, r])
            for u in range(2):
                s3d[s, u] = (sumod[u] + rod[r, u].astype(F32)).astype(BF16)
            for copy in across_copies(q, 0):
                copy.start()
            wait_bytes(rogu.at[r], corecv.at[1, r])
            for u in range(2):
                for g in range(2):
                    s3gu[s, u, g] = (sumogu[g, u] + rogu[r, g, u].astype(F32)).astype(BF16)
            for copy in across_copies(q, 1):
                copy.start()

    def scatter4(q):
        s, r = q % 2, q % SLOTS
        wait_bytes(r2d.at[r], c2recv.at[0, r])
        wait_bytes(r2gu.at[r], c2recv.at[1, r])
        wait_bytes(r3d.at[r], c3recv.at[0, r])
        wait_bytes(r3gu.at[r], c3recv.at[1, r])
        total_gu = sum_gu[s] + r2gu[r].astype(F32) + r3gu[r].astype(F32)
        total_d = sum_d[s] + r2d[r].astype(F32) + r3d[r].astype(F32)

        @pl.when(q + SLOTS < ALL)
        def _():
            pl.semaphore_signal(mate_free, 1, device_id={"dp": mate * CORES + k})
            pl.semaphore_signal(across_free.at[z % 2], 1, device_id={"dp": (2 - side) * CORES + k})

        total_gu, total_d = total_gu.astype(BF16), total_d.astype(BF16)
        layer, c = LAYERS - 1 - q // CHUNKS, q % CHUNKS
        for g in range(2):
            ggu_out[layer, g, :, pl.ds(pl.multiple_of(c * CHUNK, CHUNK), CHUNK)] = total_gu[g]
        gd_out[layer, c] = total_d
        wide_gu, wide_d = total_gu.astype(F32), total_d.astype(F32)
        squares = (wide_gu * wide_gu).reshape(2, ROWS // 8, 8, CHUNK).sum((0, 1))
        squares_d = (wide_d * wide_d).reshape(LOCAL // 8, 8, D).sum(0)
        ssb[0] += sum(squares[:, n : n + 128] for n in range(0, CHUNK, 128)) + sum(squares_d[:, n : n + 128] for n in range(0, D, 128))

    ssb[0] = jnp.zeros((8, 128), F32)

    def layer_backward(base, q0, with_input, weights_come):
        @pl.loop(0, CHUNKS)
        def _(c):
            i, q = base + c, q0 + c
            if weights_come:
                arrived(i)

            @pl.loop(0, TILES)
            def _(t):
                if weights_come:
                    gather_on(i, t)
                pl.when((t == 0) & (q >= 3))(lambda: scatter4(q - 3))
                pl.when((t == 1) & (q >= 2))(lambda: scatter3(q - 2))
                pl.when((t == 1) & (q >= 1))(lambda: scatter2(q - 1))
                backward(i, t, q % 2, with_input)

            scatter1(q)

    layer_backward(CHUNKS, 0, True, True)

    @pl.loop(0, TILES)
    def _(t):
        wide = xb[tokens(t)].astype(F32)
        by_a = acc[tokens(t)].astype(BF16).astype(F32)
        scale = norm_scale(wide)
        inner = jnp.mean(wide * by_a, -1, keepdims=True)
        by_h = by_a * scale - wide * (scale * scale * scale * inner)
        dyb[tokens(t)] = dyb[tokens(t)] + by_h.astype(BF16)
        fetch(x_hbm, xb, xsem, t).start()

    @pl.loop(0, TILES)
    def _(t):
        fetch(x_hbm, xb, xsem, t).wait()
        wide = xb[tokens(t)].astype(F32)
        abuf[tokens(t)] = (wide * norm_scale(wide)).astype(BF16)

    layer_backward(0, CHUNKS, False, False)
    scatter4(ALL - 3)
    scatter3(ALL - 2)
    scatter2(ALL - 1)
    scatter4(ALL - 2)
    scatter3(ALL - 1)
    scatter4(ALL - 1)

    def square_copy(o):
        return pltpu.make_async_remote_copy(ssb.at[0], ssb.at[o], sssend.at[o - 1], ssrecv.at[o - 1], device_id={"dp": (me + o) % GROUP})

    for o in range(1, GROUP):
        square_copy(o).start()
    for o in range(1, GROUP):
        square_copy(o).wait()
    ss_out[...] = sum(ssb[o] for o in range(GROUP))

    for q in (ALL - 2, ALL - 1):
        for copy in mate_copies(q):
            copy.wait_send()

        @pl.when(middle)
        def _(q=q):
            for copy in across_copies(q, 0) + across_copies(q, 1):
                copy.wait_send()

        @pl.when(jnp.logical_not(middle))
        def _(q=q):
            for copy in end_copies(q):
                copy.wait_send()
    wait_bytes(wgu.at[:, 0, pl.ds(0, LINE - 1), 0, 0], a1send.at[0])
    wait_bytes(wd.at[:, pl.ds(0, LINE - 1), 0, 0, :, pl.ds(0, D // 2)], a1send.at[1])
    sent = ALL * (REPS - 1) * (LINE - 1)
    wait_bytes(abuf.at[pl.ds(0, sent * HALF * CHUNK // D)], a2send.at[0])
    wait_bytes(abuf.at[pl.ds(0, sent * LOCAL // 4)], a2send.at[1])
    wait_bytes(wgu.at[:, :, :, 0], a3send.at[0])
    wait_bytes(wd.at[:, :, 0], a3send.at[1])


def gradients(x, dy, gu, down):
    vm, dma = pltpu.VMEM, pltpu.SemaphoreType.DMA
    flops = 17 * 2 * TOKENS * D * FF
    return pl.pallas_call(
        kernel,
        out_shape=(
            jax.ShapeDtypeStruct((LAYERS, 2, ROWS, FF), BF16),
            jax.ShapeDtypeStruct((LAYERS, CHUNKS, LOCAL, D), BF16),
            jax.ShapeDtypeStruct((8, 128), F32),
        ),
        in_specs=[pl.BlockSpec(memory_space=pl.ANY)] * 4,
        out_specs=(pl.BlockSpec(memory_space=pltpu.VMEM),) * 3,
        scratch_shapes=[
            vm((TOKENS, D), BF16), vm((TOKENS, D), BF16), vm((TOKENS, D), BF16), vm((TOKENS, D), F32),
            vm((ALL, 2, LINE, CORES, 2, HALF, CHUNK), BF16), vm((ALL, LINE, CORES, 2, LOCAL // 2, D), BF16),
            vm((2, 2, LINE, CORES, ROWS, CHUNK), F32), vm((2, LINE, CORES, LOCAL, D), F32),
            vm((2, LINE, ROWS, CHUNK), BF16), vm((LINE, LOCAL, D), BF16),
            vm((2, 2, LINE, ROWS, CHUNK), BF16), vm((2, LINE, LOCAL, D), BF16),
            vm((2, 2, ROWS, CHUNK), F32), vm((2, LOCAL, D), F32),
            vm((2, 2, ROWS, CHUNK), BF16), vm((2, LOCAL, D), BF16), vm((SLOTS, 2, ROWS, CHUNK), BF16), vm((SLOTS, LOCAL, D), BF16),
            vm((2, 2, 2, ROWS, CHUNK), BF16), vm((2, 2, LOCAL, D), BF16), vm((SLOTS, 2, 2, ROWS, CHUNK), BF16), vm((SLOTS, 2, LOCAL, D), BF16),
            vm((2, 2, ROWS, CHUNK), F32), vm((2, LOCAL, D), F32),
            vm((2, 2, 2, ROWS, CHUNK), BF16), vm((2, 2, LOCAL, D), BF16), vm((SLOTS, 2, ROWS, CHUNK), BF16), vm((SLOTS, LOCAL, D), BF16),
            vm((GROUP, 8, 128), F32),
            dma((TILES,)), dma((TILES,)), dma((2, ALL)), dma((2,)), dma((2, ALL)), dma((2,)), dma((2, ALL)), dma((2,)), dma((2, ALL)),
            dma((2,)), dma((2, 2)), dma((2, 2)), dma((2, SLOTS)), dma((2, 2)), dma((2, SLOTS)), dma((2, 2, 2)), dma((2, SLOTS)),
            pltpu.SemaphoreType.REGULAR, pltpu.SemaphoreType.REGULAR((2,)), dma((GROUP - 1,)), dma((GROUP - 1,)),
        ],
        compiler_params=pltpu.CompilerParams(collective_id=0, has_side_effects=True, vmem_limit_bytes=67043328),
        cost_estimate=pl.CostEstimate(flops=flops, bytes_accessed=2 * TOKENS * D * 2, transcendentals=0),
    )(x, dy, gu, down)


def solution(mesh):
    def step(x, dy, w_gate, w_up, w_down, m_gate, m_up, m_down, v_gate, v_up, v_down):
        own = lax.optimization_barrier(jnp.asarray(ORDER))
        order = (lax.broadcasted_iota(jnp.int32, (FF, FF), 0) == own[None, :]).astype(BF16)
        gu = jnp.stack([w_gate, w_up], 1)
        placed = jnp.dot(gu.reshape(-1, FF), order, preferred_element_type=F32).astype(BF16)
        ggu, gd, squares = gradients(
            x, dy, placed.reshape(LAYERS, 2, 2, HALF, FF), w_down.reshape(LAYERS, CHUNKS, 2, LOCAL // 2, D)
        )
        ggu = lax.dot_general(ggu.reshape(-1, FF), order, (((1,), (1,)), ((), ())), preferred_element_type=F32)
        ggu = ggu.astype(BF16).astype(F32).reshape(LAYERS, 2, ROWS, FF)
        g = [ggu[:, 0], ggu[:, 1], gd.reshape(w_down.shape).astype(F32)]
        count = GROUP * sum(one.size for one in g)
        factor = jnp.minimum(1.0, 0.5 * lax.rsqrt(jnp.sum(squares) / count + 1e-30))
        new = [
            adamw(w.astype(F32), m, v, one * factor)
            for w, m, v, one in zip((w_gate, w_up, w_down), (m_gate, m_up, m_down), (v_gate, v_up, v_down), g, strict=True)
        ]
        return tuple(one[which] for which in range(3) for one in new)

    states, cut = P(("rep", "dp"), None, None), P(None, "dp", None)
    return jax.shard_map(
        step,
        mesh=mesh,
        in_specs=(states, states) + (cut,) * 9,
        out_specs=(P("rep", "dp", None),) * 9,
        check_vma=False,
    )
```

time: 344 us -> 307 us (0.89)
  Pallas kernels: 320 us -> 281 us
    pallas_call x1, Pallas kernels: 320 us -> 281 us  [gradients(): pl.pallas_call(kernel, out_shape=(jax.ShapeDtypeStruct((LAYERS, 2, ROWS,...]
where the time goes in v2:
time: 307 us; the launch traced here: 306 us
  Pallas kernels  281 us (92%)
  other arithmetic  11 us (4%)
  matrix products  10.8 us (4%)
    pallas_call x1, Pallas kernels, gradients(): pl.pallas_call(kernel, out_shape=(jax.ShapeDtypeStruct((LAYERS, 2, ROWS,...  281 us
    convert_element_type x2, other arithmetic, adamw(): return ((w - 0.02 * step).astype(BF16), m, v)  8.61 us
    dot_general x1, matrix products, step(): jnp.dot(gu.reshape(-1, FF), order, preferred_element_type=F32).astype(BF16)  6.64 us

profile of v2, /device:TPU:0, one launch (start us, length us, event | category | flops | bytes accessed | tf_op | source)
XLA Modules:
  0.0 306.3 jit_solution(17882973770280815201)
XLA Ops:
  0.6 0.0 copy-start.6
  0.7 1.4 pad_maximum_fusion
  2.1 0.0 copy-done.6
  2.1 6.6 %fusion.4 = bf16[384,1792]{1,0:T(8,128)(2,1)} fusion(bf16[384,1792]{1,0:T(8,128)(2,1)S(1)} %bitcast.60, s32[1792]{0:T(1024)S(1)} %copy-done.6), kind=kOutput, calls=%fused_computation.5 | convolution fusion | flops 2470150144 | bytes 2759680 | tf_op jit(solution)/shard_map/dot_general | solution.py:425
  8.8 281.3 %shard_map.187 = (bf16[2,2,96,1792]{3,2,1,0:T(8,128)(2,1)}, bf16[2,7,32,768]{3,2,1,0:T(8,128)(2,1)}, f32[8,128]{1,0:T(8,128)}) custom-call(bf16[1,4096,768]{2,1,0:T(8,128)(2,1)} %x_hbm.1, bf16[1,4096,768]{2,1,0:T(8,128)(2,1)} %dy_hbm.1, bf16[2,2,2,48,1792]{4,3,2,1,0:T(8,128)(2,1)} %bitcast.63, bf16[2,7,2,16,768]{4,3,2,1,0:T(8,128)(2,1)} %bitcast.61), custom_call_target="tpu_custom_call" | custom-call | flops 191662915584 | bytes 12582912 | tf_op jit(solution)/shard_map/pallas_call | solution.py:390
  290.0 4.1 %fusion.5 = bf16[384,1792]{1,0:T(8,128)(2,1)S(1)} fusion(bf16[384,1792]{1,0:T(8,128)(2,1)} %bitcast.62, s32[1792]{0:T(1024)} %constant.7.clone), kind=kOutput, calls=%fused_computation.6 | convolution fusion | flops 2470150144 | bytes 2759680 | tf_op jit(solution)/shard_map/dot_general | solution.py:429
  294.2 0.0 copy-start.5
  294.2 0.0 copy-start
  294.2 0.2 convert.1
  294.4 0.4 copy-done.5
  294.9 0.6 reduce_sum.9
  296.1 0.0 copy-done
  296.2 0.0 copy-start.3
  296.2 0.0 copy-start.2
  296.2 6.5 %fusion.11 = (bf16[2,96,1792]{2,1,0:T(8,128)(2,1)}, f32[2,96,1792]{2,1,0:T(8,128)}, f32[2,96,1792]{2,1,0:T(8,128)}, bf16[2,96,1792]{2,1,0:T(8,128)(2,1)}, f32[2,96,1792]{2,1,0:T(8,128)}, /*index=5*/f32[2,96,1792]{2,1,0:T(8,128)}) fusion(bf16[2,96,1792]{2,1,0:T(8,128)(2,1)S(1)} %copy-done, f32[]{:T(128)S(6)} %min_shard_map.3, ...), kind=kLoop, calls=%fused_computation.21 | loop fusion | flops 11010048 | bytes 16515076 | tf_op jit(solution)/shard_map/convert_element_type | solution.py:32
  302.7 0.0 copy-start.1
  302.7 0.0 copy-start.4
  302.7 0.0 copy-done.3
  302.7 0.1 convert_multiply_fusion.3
  302.8 0.0 copy-done.2
  302.8 1.2 copy-done.1
  304.0 0.2 copy-done.4
  304.2 2.1 fusion.14
Async XLA Ops:
  0.6 1.5 copy-start.6
  294.2 0.7 copy-start.5
  294.2 2.0 copy-start
  296.2 6.5 %copy-start.3 = (bf16[2,7,32,768]{3,2,1,0:T(8,128)(2,1)S(1)}, bf16[2,7,32,768]{3,2,1,0:T(8,128)(2,1)}, u32[]{:S(2)}) copy-start(bf16[2,7,32,768]{3,2,1,0:T(8,128)(2,1)} %get-tuple-element.14) | copy-start | bytes 2064388
  296.2 6.7 %copy-start.2 = (f32[2,224,768]{2,1,0:T(8,128)S(1)}, f32[2,224,768]{2,1,0:T(8,128)}, u32[]{:S(2)}) copy-start(f32[2,224,768]{2,1,0:T(8,128)} %param.19) | copy-start | bytes 4128772
  302.7 1.3 copy-start.1
  302.7 1.5 copy-start.4

commit v3 on v2

--- a/solution.py
+++ b/solution.py
@@ -2,7 +2,6 @@
 
 import jax
 import jax.numpy as jnp
-import numpy as np
 from jax import lax
 from jax.experimental import pallas as pl
 from jax.experimental.pallas import tpu as pltpu
@@ -22,7 +21,6 @@
 SLOTS = 3
 ALL = LAYERS * CHUNKS
 F32, BF16 = jnp.float32, jnp.bfloat16
-ORDER = np.arange(FF, dtype=np.int32).reshape(GROUP, CHUNKS, LOCAL).transpose(1, 0, 2).reshape(FF)
 
 
 def adamw(w, m, v, g):
@@ -41,10 +39,10 @@
 
 
 def kernel(
-    x_hbm, dy_hbm, gu_hbm, d_hbm, ggu_out, gd_out, ss_out,
-    abuf, xb, dyb, acc, wgu, wd, gg, gd,
+    x_hbm, dy_hbm, gate_hbm, up_hbm, d_hbm, gate_out, up_out, gd_out, ss_out,
+    placed, abuf, xb, dyb, acc, wgu, wd, gg, gd,
     s1gu, s1d, r1gu, r1d, sum_gu, sum_d, s2gu, s2d, r2gu, r2d, sogu, sod, rogu, rod, sumogu, sumod, s3gu, s3d, r3gu, r3d, ssb,
-    xsem, dysem, ownsem, a1send, a1recv, a2send, a2recv, a3send, a3recv,
+    xsem, dysem, gusem, ownsem, a1send, a1recv, a2send, a2recv, a3send, a3recv,
     c1send, c1recv, c2send, c2recv, cosend, corecv, c3send, c3recv, mate_free, across_free, sssend, ssrecv,
 ):
     rep, me = lax.axis_index("rep"), lax.axis_index("dp")
@@ -64,9 +62,27 @@
     def fetch(hbm, vmem, sem, t):
         return pltpu.make_async_copy(hbm.at[0, tokens(t)], vmem.at[tokens(t)], sem.at[t])
 
+    raw = [pltpu.make_async_copy(hbm, placed.at[:, g], gusem.at[0, g]) for g, hbm in enumerate((gate_hbm, up_hbm))]
+    for copy in raw:
+        copy.start()
     for t in range(TILES):
         fetch(x_hbm, xb, xsem, t).start()
         fetch(dy_hbm, dyb, dysem, t).start()
+
+    def chosen(c):
+        place = lax.broadcasted_iota(jnp.int32, (1, CHUNK), 1)
+        column = place // LOCAL * (FF // GROUP) + place % LOCAL + c * LOCAL
+        return jnp.where(lax.broadcasted_iota(jnp.int32, (FF, CHUNK), 0) == column, 1.0, 0.0).astype(BF16)
+
+    def place(c):
+        columns = dot(placed[...].reshape(LAYERS * 2 * ROWS, FF), chosen(c)).astype(BF16).reshape(LAYERS, 2, 2, HALF, CHUNK)
+        for layer in range(LAYERS):
+            for g in range(2):
+                wgu[layer * CHUNKS + c, g, z, k] = columns[layer, g]
+
+    for copy in raw:
+        copy.wait()
+    place(0)
     pl.semaphore_wait(barrier, GROUP - 1 + REPS - 1)
 
     def wait_bytes(ref, sem):
@@ -79,15 +95,13 @@
 
     def gather1(i):
         layer, c = i // CHUNKS, i % CHUNKS
-        columns = pl.ds(pl.multiple_of(c * CHUNK, CHUNK), CHUNK)
-        gu, down = gu_hbm.at[layer, rg, rh, :, columns], d_hbm.at[layer, c, rg, :, d_half]
         gu_to, d_to = quarter(i, z)
+        gu, down = gu_to, d_hbm.at[layer, c, rg, :, d_half]
         for o in range(1, LINE):
             to = {"dp": (z + o) % LINE * CORES + k}
             pltpu.make_async_remote_copy(gu, gu_to, a1send.at[0], a1recv.at[0, i], device_id=to).start()
             pltpu.make_async_remote_copy(down, d_to, a1send.at[1], a1recv.at[1, i], device_id=to).start()
-        pltpu.make_async_copy(gu_hbm.at[layer, :, :, :, columns], wgu.at[i, :, z, k], ownsem.at[0, i]).start()
-        pltpu.make_async_copy(d_hbm.at[layer, c], wd.at[i, z, k], ownsem.at[1, i]).start()
+        pltpu.make_async_copy(d_hbm.at[layer, c], wd.at[i, z, k], ownsem.at[i]).start()
 
     def gather2(i):
         wait_bytes(wgu.at[i, 0, pl.ds(0, LINE - 1), 0, 0], a1recv.at[0, i])
@@ -102,8 +116,7 @@
     def gather3(i):
         wait_bytes(wgu.at[pl.ds(0, REPS - 1), 0, pl.ds(0, LINE - 1), 0, 0], a2recv.at[0, i])
         wait_bytes(wd.at[pl.ds(0, REPS - 1), pl.ds(0, LINE - 1), 0, 0, :, pl.ds(0, D // 2)], a2recv.at[1, i])
-        wait_bytes(wgu.at[i, :, 0, 0], ownsem.at[0, i])
-        wait_bytes(wd.at[i, 0, 0], ownsem.at[1, i])
+        wait_bytes(wd.at[i, 0, 0], ownsem.at[i])
         gu, down = wgu.at[i, :, :, k], wd.at[i, :, k]
         to = {"dp": z * CORES + other}
         pltpu.make_async_remote_copy(gu, gu, a3send.at[0], a3recv.at[0, i], device_id=to).start()
@@ -114,21 +127,29 @@
         wait_bytes(wd.at[i, :, 0], a3recv.at[1, i])
 
     def gather_on(i, t):
+        pl.when((t == 0) & (i == 0))(lambda: gather2(2))
         pl.when((t == 1) & (i + AHEAD < ALL))(lambda: gather1(i + AHEAD))
-        pl.when((t == 1) & (i + 2 < ALL))(lambda: gather2(i + 2))
         pl.when((t == 2) & (i + 1 < ALL))(lambda: gather3(i + 1))
-
-    pl.loop(0, AHEAD)(gather1)
-    acc[...] = jnp.zeros_like(acc)
-
-    @pl.loop(0, TILES)
-    def _(t):
+        pl.when((t == 3) & (i + 3 < ALL))(lambda: gather2(i + 3))
+
+    gather1(0)
+
+    @pl.loop(1, AHEAD)
+    def _(c):
+        place(c)
+        gather1(c)
+
+    def norm_tile(t):
         fetch(x_hbm, xb, xsem, t).wait()
         wide = xb[tokens(t)].astype(F32)
         abuf[tokens(t)] = (wide * norm_scale(wide)).astype(BF16)
 
+    pl.loop(0, TILES // 2)(norm_tile)
     gather2(0)
+    pl.loop(AHEAD, CHUNKS)(place)
+    acc[...] = jnp.zeros_like(acc)
     gather2(1)
+    pl.loop(TILES // 2, TILES)(norm_tile)
     gather3(0)
 
     def weights(i):
@@ -139,14 +160,16 @@
     def _(c):
         arrived(c)
 
-        @pl.loop(0, TILES)
+        @pl.loop(0, TILES // 2)
         def _(t):
-            gather_on(c, t)
+            gather_on(c, 2 * t)
+            gather_on(c, 2 * t + 1)
+            there = pl.ds(pl.multiple_of(t * 2 * TILE, 2 * TILE), 2 * TILE)
             wg, wu, down = weights(c)
-            a = abuf[tokens(t)]
+            a = abuf[there]
             gate, up = dot(a, wg), dot(a, wu)
             hidden = (gate * jax.nn.sigmoid(gate) * up).astype(BF16)
-            acc[tokens(t)] += dot(hidden, down)
+            acc[there] += dot(hidden, down)
 
     @pl.loop(0, TILES)
     def _(t):
@@ -300,12 +323,31 @@
         total_gu, total_d = total_gu.astype(BF16), total_d.astype(BF16)
         layer, c = LAYERS - 1 - q // CHUNKS, q % CHUNKS
         for g in range(2):
-            ggu_out[layer, g, :, pl.ds(pl.multiple_of(c * CHUNK, CHUNK), CHUNK)] = total_gu[g]
+            placed[layer, g, :, pl.ds(pl.multiple_of(c * CHUNK, CHUNK), CHUNK)] = total_gu[g]
         gd_out[layer, c] = total_d
         wide_gu, wide_d = total_gu.astype(F32), total_d.astype(F32)
         squares = (wide_gu * wide_gu).reshape(2, ROWS // 8, 8, CHUNK).sum((0, 1))
         squares_d = (wide_d * wide_d).reshape(LOCAL // 8, 8, D).sum(0)
         ssb[0] += sum(squares[:, n : n + 128] for n in range(0, CHUNK, 128)) + sum(squares_d[:, n : n + 128] for n in range(0, D, 128))
+
+    def block(layer, n):
+        return acc.at[pl.ds((layer * 3 + n // 3) * 2 * ROWS, 2 * ROWS), n % 3 * CHUNK : (n % 3 + 1) * CHUNK]
+
+    def put_back(layer, c):
+        columns = placed[layer, :, :, pl.ds(pl.multiple_of(c * CHUNK, CHUNK), CHUNK)].reshape(2 * ROWS, CHUNK)
+        to = chosen(c)
+        for n in range(CHUNKS):
+            there = block(layer, n)
+            there[...] = jnp.where(c == 0, 0.0, there[...]) + dot(columns, to[n * CHUNK : (n + 1) * CHUNK], 1, 1)
+
+    def out_copies(layer):
+        return [pltpu.make_async_copy(placed.at[layer, g], out.at[layer], gusem.at[layer, g]) for g, out in enumerate((gate_out, up_out))]
+
+    def put_out(layer):
+        for n in range(CHUNKS):
+            placed[layer, :, :, n * CHUNK : (n + 1) * CHUNK] = block(layer, n)[...].astype(BF16).reshape(2, ROWS, CHUNK)
+        for copy in out_copies(layer):
+            copy.start()
 
     ssb[0] = jnp.zeros((8, 128), F32)
 
@@ -349,8 +391,11 @@
     scatter4(ALL - 3)
     scatter3(ALL - 2)
     scatter2(ALL - 1)
+    pl.loop(0, CHUNKS)(lambda c: put_back(1, c))
+    put_out(1)
     scatter4(ALL - 2)
     scatter3(ALL - 1)
+    pl.loop(0, CHUNKS - 1)(lambda c: put_back(0, c))
     scatter4(ALL - 1)
 
     def square_copy(o):
@@ -358,9 +403,15 @@
 
     for o in range(1, GROUP):
         square_copy(o).start()
+    put_back(0, CHUNKS - 1)
+    put_out(0)
     for o in range(1, GROUP):
         square_copy(o).wait()
-    ss_out[...] = sum(ssb[o] for o in range(GROUP))
+    ss_out[0, 0] = jnp.sum(sum(ssb[o] for o in range(GROUP)))
+
+    for layer in range(LAYERS):
+        for copy in out_copies(layer):
+            copy.wait()
 
     for q in (ALL - 2, ALL - 1):
         for copy in mate_copies(q):
@@ -384,19 +435,21 @@
     wait_bytes(wd.at[:, :, 0], a3send.at[1])
 
 
-def gradients(x, dy, gu, down):
+def gradients(x, dy, gate, up, down):
     vm, dma = pltpu.VMEM, pltpu.SemaphoreType.DMA
     flops = 17 * 2 * TOKENS * D * FF
     return pl.pallas_call(
         kernel,
         out_shape=(
-            jax.ShapeDtypeStruct((LAYERS, 2, ROWS, FF), BF16),
+            jax.ShapeDtypeStruct((LAYERS, ROWS, FF), BF16),
+            jax.ShapeDtypeStruct((LAYERS, ROWS, FF), BF16),
             jax.ShapeDtypeStruct((LAYERS, CHUNKS, LOCAL, D), BF16),
-            jax.ShapeDtypeStruct((8, 128), F32),
+            jax.ShapeDtypeStruct((1, 1), F32),
         ),
-        in_specs=[pl.BlockSpec(memory_space=pl.ANY)] * 4,
-        out_specs=(pl.BlockSpec(memory_space=pltpu.VMEM),) * 3,
+        in_specs=[pl.BlockSpec(memory_space=pl.ANY)] * 5,
+        out_specs=(pl.BlockSpec(memory_space=pl.ANY),) * 2 + (pl.BlockSpec(memory_space=pltpu.VMEM), pl.BlockSpec(memory_space=pltpu.SMEM)),
         scratch_shapes=[
+            vm((LAYERS, 2, ROWS, FF), BF16),
             vm((TOKENS, D), BF16), vm((TOKENS, D), BF16), vm((TOKENS, D), BF16), vm((TOKENS, D), F32),
             vm((ALL, 2, LINE, CORES, 2, HALF, CHUNK), BF16), vm((ALL, LINE, CORES, 2, LOCAL // 2, D), BF16),
             vm((2, 2, LINE, CORES, ROWS, CHUNK), F32), vm((2, LINE, CORES, LOCAL, D), F32),
@@ -408,31 +461,23 @@
             vm((2, 2, ROWS, CHUNK), F32), vm((2, LOCAL, D), F32),
             vm((2, 2, 2, ROWS, CHUNK), BF16), vm((2, 2, LOCAL, D), BF16), vm((SLOTS, 2, ROWS, CHUNK), BF16), vm((SLOTS, LOCAL, D), BF16),
             vm((GROUP, 8, 128), F32),
-            dma((TILES,)), dma((TILES,)), dma((2, ALL)), dma((2,)), dma((2, ALL)), dma((2,)), dma((2, ALL)), dma((2,)), dma((2, ALL)),
+            dma((TILES,)), dma((TILES,)), dma((LAYERS, 2)), dma((ALL,)), dma((2,)), dma((2, ALL)), dma((2,)), dma((2, ALL)), dma((2,)), dma((2, ALL)),
             dma((2,)), dma((2, 2)), dma((2, 2)), dma((2, SLOTS)), dma((2, 2)), dma((2, SLOTS)), dma((2, 2, 2)), dma((2, SLOTS)),
             pltpu.SemaphoreType.REGULAR, pltpu.SemaphoreType.REGULAR((2,)), dma((GROUP - 1,)), dma((GROUP - 1,)),
         ],
         compiler_params=pltpu.CompilerParams(collective_id=0, has_side_effects=True, vmem_limit_bytes=67043328),
         cost_estimate=pl.CostEstimate(flops=flops, bytes_accessed=2 * TOKENS * D * 2, transcendentals=0),
-    )(x, dy, gu, down)
+    )(x, dy, gate, up, down)
 
 
 def solution(mesh):
     def step(x, dy, w_gate, w_up, w_down, m_gate, m_up, m_down, v_gate, v_up, v_down):
-        own = lax.optimization_barrier(jnp.asarray(ORDER))
-        order = (lax.broadcasted_iota(jnp.int32, (FF, FF), 0) == own[None, :]).astype(BF16)
-        gu = jnp.stack([w_gate, w_up], 1)
-        placed = jnp.dot(gu.reshape(-1, FF), order, preferred_element_type=F32).astype(BF16)
-        ggu, gd, squares = gradients(
-            x, dy, placed.reshape(LAYERS, 2, 2, HALF, FF), w_down.reshape(LAYERS, CHUNKS, 2, LOCAL // 2, D)
-        )
-        ggu = lax.dot_general(ggu.reshape(-1, FF), order, (((1,), (1,)), ((), ())), preferred_element_type=F32)
-        ggu = ggu.astype(BF16).astype(F32).reshape(LAYERS, 2, ROWS, FF)
-        g = [ggu[:, 0], ggu[:, 1], gd.reshape(w_down.shape).astype(F32)]
+        g_gate, g_up, g_down, squares = gradients(x, dy, w_gate, w_up, w_down.reshape(LAYERS, CHUNKS, 2, LOCAL // 2, D))
+        g = [g_gate, g_up, g_down.reshape(w_down.shape)]
         count = GROUP * sum(one.size for one in g)
-        factor = jnp.minimum(1.0, 0.5 * lax.rsqrt(jnp.sum(squares) / count + 1e-30))
+        factor = jnp.minimum(1.0, 0.5 * lax.rsqrt(squares.reshape(()) / count + 1e-30))
         new = [
-            adamw(w.astype(F32), m, v, one * factor)
+            adamw(w.astype(F32), m, v, one.astype(F32) * factor)
             for w, m, v, one in zip((w_gate, w_up, w_down), (m_gate, m_up, m_down), (v_gate, v_up, v_down), g, strict=True)
         ]
         return tuple(one[which] for which in range(3) for one in new)

time: 307 us -> 292 us (0.951)
  matrix products: 10.8 us -> 0 us
    dot_general x2 -> x0, matrix products: 10.8 us -> none  [the longest x1 6.64 us: step(): jnp.dot(gu.reshape(-1, FF), order, preferred_element_type=F32).astype(BF16)]
where the time goes in v3:
time: 292 us
  Pallas kernels  280 us (96%)
  other arithmetic  9.34 us (3%)
    pallas_call x1, Pallas kernels, gradients(): pl.pallas_call(kernel, out_shape=(jax.ShapeDtypeStruct((LAYERS, ROWS, FF)...  280 us
    convert_element_type x2, other arithmetic, adamw(): return ((w - 0.02 * step).astype(BF16), m, v)  9.21 us

profile of v3, /device:TPU:0, one launch (start us, length us, event | category | flops | bytes accessed | tf_op | source)
XLA Modules:
  0.0 292.2 jit_solution(1902672952886811119)
XLA Ops:
  0.6 280.2 %shard_map.178 = (bf16[2,96,1792]{2,1,0:T(8,128)(2,1)}, bf16[2,96,1792]{2,1,0:T(8,128)(2,1)}, bf16[2,7,32,768]{3,2,1,0:T(8,128)(2,1)}, f32[1,1]{1,0:T(1,128)}) custom-call(bf16[1,4096,768]{2,1,0:T(8,128)(2,1)} %x_hbm.1, bf16[1,4096,768]{2,1,0:T(8,128)(2,1)} %dy_hbm.1, bf16[2,96,1792]{2,1,0:T(8,128)(2,1)} %gate_hbm.1, bf16[2,96,1792]{2,1,0:T(8,128)(2,1)} %up_hbm.1, ...), custom_call_target="tpu_custom_call" | custom-call | flops 191662915584 | bytes 12582912 | tf_op jit(solution)/shard_map/pallas_call | solution.py:441
  281.5 0.0 copy-start.2
  281.5 0.0 copy-start.1
  281.5 7.1 %fusion.2 = (bf16[2,96,1792]{2,1,0:T(8,128)(2,1)}, f32[2,96,1792]{2,1,0:T(8,128)}, f32[2,96,1792]{2,1,0:T(8,128)}, bf16[2,96,1792]{2,1,0:T(8,128)(2,1)}, f32[2,96,1792]{2,1,0:T(8,128)}, /*index=5*/f32[2,96,1792]{2,1,0:T(8,128)}) fusion(bf16[2,96,1792]{2,1,0:T(8,128)(2,1)} %gate_hbm.1, f32[]{:T(128)} %bitcast.1, bf16[2,96,1792]{2,1,0:T(8,128)(2,1)} %get-tuple-element.13, ...), kind=kLoop, calls=%fused_computation.11 | loop fusion | flops 11698176 | bytes 15138820 | tf_op jit(solution)/shard_map/convert_element_type | solution.py:30
  288.6 0.0 copy-start
  288.6 0.0 copy-start.3
  288.6 0.0 copy-done.2
  288.6 0.1 convert_multiply_fusion.3
  288.8 0.0 copy-done.1
  288.8 1.2 copy-done
  290.0 0.2 copy-done.3
  290.1 2.1 fusion.8
Async XLA Ops:
  281.5 7.2 %copy-start.2 = (bf16[2,7,32,768]{3,2,1,0:T(8,128)(2,1)S(1)}, bf16[2,7,32,768]{3,2,1,0:T(8,128)(2,1)}, u32[]{:S(2)}) copy-start(bf16[2,7,32,768]{3,2,1,0:T(8,128)(2,1)} %get-tuple-element.16) | copy-start | bytes 2064388
  281.5 7.3 %copy-start.1 = (f32[2,224,768]{2,1,0:T(8,128)S(1)}, f32[2,224,768]{2,1,0:T(8,128)}, u32[]{:S(2)}) copy-start(f32[2,224,768]{2,1,0:T(8,128)} %param.18) | copy-start | bytes 4128772
  288.6 1.3 copy-start
  288.6 1.5 copy-start.3
